TPU v7x, 32 devices: a whole 2x2x4 slice. The times are simulated.
32 devices in a mesh: pix: 8 (over y, x, core), tm: 4 (over z).
Axes of the slice: x: 2, y: 2, z: 4, core: 2. Of those that a mesh axis runs over, the one named last changes fastest.
Arguments:
- recording: bfloat16 [128, 256, 512], P('pix', None, 'tm'), may hold values from 0 to 12, as said below
- footprints: float32 [128, 2, 256, 128], P('pix'), may hold values from 0 to 0.03
- traces: float32 [96, 128, 512], P(None, None, 'tm'), may hold values from 0 to 1
- block_list: int32 [128, 2], P('pix'), may hold values from 0 to 95, as said below
- block_order: int32 [96], replicated, may hold values from 0 to 95, as said below
Outputs:
- footprints_out: float32 [128, 2, 256, 128], P('pix')
- traces_out: float32 [96, 128, 512], P(None, None, 'tm')
Inputs may be any that keep to these rules, and one draw needn't show every extreme that they name: `recording`: nonnegative intensities. block_list[p, g] is one of block_order[g * 48] to block_order[(g + 1) * 48 - 1], and every block is named by some patch. `block_order`: a permutation of the component blocks.
All inputs are finite; a program needn't handle non-finite values.
Results may differ from a plain program's by a relative error of at most 0.0003.
Values sent between devices are 32-bit elements; how exact they have to be, the bound alone decides.
No kernel may reach another device: no remote copies, remote signals or barrier semaphores. Data moves between devices by JAX's collectives and lax.ppermute only.
A program may use at most 128 MiB of HBM per device.

v0:
```python
import jax
import jax.numpy as jnp
from jax import lax
from jax.sharding import PartitionSpec as P

KB = 128
GROUPS = 2
BPG = 48
SWEEPS = 2


epsilon = 1e-06


def product(form, left, right):
    return jnp.einsum(form, left, right, precision=lax.Precision.HIGHEST)


def member_table(block_list, block_order, group_index):
    chosen = block_order[group_index * BPG : (group_index + 1) * BPG]
    member = (block_list[:, group_index][:, None] == chosen[None, :]).astype(jnp.float32)
    return (member, chosen)


def local(recording, footprints, traces, block_list, block_order):
    residual = recording.astype(jnp.float32)
    for group_index in range(GROUPS):
        current = jnp.take(traces, block_list[:, group_index], axis=0)
        residual = residual - product("pvk,pkf->pvf", footprints[:, group_index], current)
    for sweep_index in range(SWEEPS):
        tables = [
            member_table(block_list, block_order, group_index) for group_index in range(GROUPS)
        ]
        partial_norms = jnp.stack(
            [
                product(
                    "pj,pk->jk",
                    tables[group_index][0],
                    jnp.sum(footprints[:, group_index] * footprints[:, group_index], axis=1),
                )
                for group_index in range(GROUPS)
            ],
            axis=0,
        )
        norms = lax.psum(partial_norms, "pix")
        for group_index in range(GROUPS):
            member, chosen = tables[group_index]
            local_terms = product("pvk,pvf->pkf", footprints[:, group_index], residual)
            partial_totals = product("pj,pkf->jkf", member, local_terms)
            before = jnp.take(traces, chosen, axis=0)
            totals = lax.psum(partial_totals, "pix")
            after = jnp.maximum(
                before + totals / (KB * norms[group_index][:, :, None] + epsilon), 0.0
            )
            traces = traces.at[chosen].set(after)
            change = product("pj,jkf->pkf", member, after - before)
            residual = residual - product("pvk,pkf->pvf", footprints[:, group_index], change)
        energy = lax.psum(jnp.sum(traces * traces, axis=2), "tm")
        for group_index in range(GROUPS):
            current = jnp.take(traces, block_list[:, group_index], axis=0)
            partial_weights = product("pvf,pkf->pvk", residual, current)
            weights = lax.psum_scatter(partial_weights, "tm", scatter_dimension=0, tiled=True)
            patch_count = weights.shape[0]
            first_patch = lax.axis_index("tm") * patch_count
            previous = footprints[:, group_index]
            old_patches = lax.dynamic_slice_in_dim(previous, first_patch, patch_count, 0)
            scale = jnp.take(energy, block_list[:, group_index], axis=0)
            scale_rows = lax.dynamic_slice_in_dim(scale, first_patch, patch_count, 0)
            new_patches = jnp.maximum(
                old_patches + weights / (KB * scale_rows[:, None, :] + epsilon), 0.0
            )
            updated = lax.all_gather(new_patches, "tm", axis=0, tiled=True)
            footprints = footprints.at[:, group_index].set(updated)
            residual = residual - product("pvk,pkf->pvf", updated - previous, current)
    return (footprints, traces)


def solution(mesh):
    in_specs = (
        P("pix", None, "tm"),
        P("pix", None, None, None),
        P(None, None, "tm"),
        P("pix", None),
        P(),
    )
    out_specs = (P("pix", None, None, None), P(None, None, "tm"))
    return jax.shard_map(local, mesh=mesh, in_specs=in_specs, out_specs=out_specs, check_vma=False)
```

profile of v0, /device:TPU:0, one launch (start us, length us, event | category | flops | bytes accessed | tf_op | source)
XLA Modules:
  0.0 841.8 jit_solution(12809691706161402841)
XLA Ops:
  7.2 6.4 copy.173
  37.6 27.2 %psum.57 = f32[2,48,128]{2,1,0:T(8,128)S(1)} all-reduce(f32[2,48,128]{2,1,0:T(8,128)S(1)} %pad_maximum_fusion), channel_id=1, replica_groups=mesh['pix'=8,'tm'=4] {'pix'}, use_global_device_ids=true, to_apply=%region_3.0 | all-reduce | flops 12288 | bytes 98304 | tf_op jit(solution)/shard_map/psum | solution.py:45
  70.2 37.3 %all-reduce.5.cloned.1.call-done = f32[48,128,128]{2,0,1:T(8,128)} async-done(((f32[48,128,128]{2,0,1:T(8,128)}), f32[48,128,128]{2,0,1:T(8,128)}) %all-reduce.5.cloned.1.call-update) | async-done | bytes 3145744 | tf_op jit(solution)/shard_map/psum | solution.py:51
  132.6 9.3 %scatter_fusion = f32[96,128,128]{2,1,0:T(8,128)} fusion(f32[96,128,128]{2,1,0:T(8,128)} %copy.173, s32[48]{0:T(128)S(1)} %get-tuple-element.78, f32[48,128,128]{2,1,0:T(8,128)} %copy.63), kind=kCustom, calls=%fused_computation.14 | custom fusion | bytes 9437376 | tf_op jit(solution)/shard_map/scatter | solution.py:55
  145.5 53.8 %all-reduce.7.cloned.1.call-done = f32[48,128,128]{2,0,1:T(8,128)} async-done(((f32[48,128,128]{2,0,1:T(8,128)}), f32[48,128,128]{2,0,1:T(8,128)}) %all-reduce.7.cloned.1.call-update) | async-done | bytes 3145744 | tf_op jit(solution)/shard_map/psum | solution.py:51
  212.6 9.0 %scatter_fusion.1 = f32[96,128,128]{2,1,0:T(8,128)} fusion(f32[96,128,128]{2,1,0:T(8,128)} %scatter_fusion, s32[48]{0:T(128)S(1)} %get-tuple-element.62, f32[48,128,128]{2,1,0:T(8,128)} %copy.68), kind=kCustom, calls=%fused_computation.15 | custom fusion | bytes 9437376 | tf_op jit(solution)/shard_map/scatter | solution.py:55
  238.5 21.4 %psum.59 = f32[96,128]{1,0:T(8,128)S(1)} all-reduce(f32[96,128]{1,0:T(8,128)S(1)} %multiply_reduce_fusion.1), channel_id=1, replica_groups=mesh['pix'=8,'tm'=4] {'tm'}, use_global_device_ids=true, to_apply=%region_9.12 | all-reduce | flops 12288 | bytes 98304 | tf_op jit(solution)/shard_map/psum | solution.py:58
  260.6 15.0 %reduce-scatter.5.cloned.1.call-done = f32[4,256,128]{2,1,0:T(8,128)} async-done(((f32[16,256,128]{2,1,0:T(8,128)}), f32[4,256,128]{2,1,0:T(8,128)}) %reduce-scatter.5.cloned.1.call-update) | async-done | bytes 524304 | tf_op jit(solution)/shard_map/reduce_scatter | solution.py:62
  282.1 40.6 %all-gather.5.cloned.1.call-done = f32[16,256,128]{2,1,0:T(8,128)} async-done(((f32[4,256,128]{2,1,0:T(8,128)}), f32[16,256,128]{2,1,0:T(8,128)}) %all-gather.5.cloned.1.call-update) | async-done | bytes 2097168 | tf_op jit(solution)/shard_map/all_gather | solution.py:72
  333.7 5.5 copy.71
  347.6 28.6 %reduce-scatter.7.cloned.1.call-done = f32[4,256,128]{2,1,0:T(8,128)} async-done(((f32[16,256,128]{2,1,0:T(8,128)}), f32[4,256,128]{2,1,0:T(8,128)}) %reduce-scatter.7.cloned.1.call-update) | async-done | bytes 524304 | tf_op jit(solution)/shard_map/reduce_scatter | solution.py:62
  378.5 44.8 %all-gather.7.cloned.1.call-done = f32[16,256,128]{2,1,0:T(8,128)} async-done(((f32[4,256,128]{2,1,0:T(8,128)}), f32[16,256,128]{2,1,0:T(8,128)}) %all-gather.7.cloned.1.call-update) | async-done | bytes 2097168 | tf_op jit(solution)/shard_map/all_gather | solution.py:72
  446.8 25.2 %psum.61 = f32[2,48,128]{2,1,0:T(8,128)S(1)} all-reduce(f32[2,48,128]{2,1,0:T(8,128)S(1)} %pad_maximum_fusion.1), channel_id=1, replica_groups=mesh['pix'=8,'tm'=4] {'pix'}, use_global_device_ids=true, to_apply=%region_14.18 | all-reduce | flops 12288 | bytes 98304 | tf_op jit(solution)/shard_map/psum | solution.py:45
  472.2 35.6 %all-reduce.9.cloned.1.call-done = f32[48,128,128]{2,0,1:T(8,128)} async-done(((f32[48,128,128]{2,0,1:T(8,128)}), f32[48,128,128]{2,0,1:T(8,128)}) %all-reduce.9.cloned.1.call-update) | async-done | bytes 3145744 | tf_op jit(solution)/shard_map/psum | solution.py:51
  507.7 5.6 add_maximum_fusion.1
  533.3 9.1 %scatter_fusion.2 = f32[96,128,128]{2,1,0:T(8,128)} fusion(f32[96,128,128]{2,1,0:T(8,128)} %scatter_fusion.1, s32[48]{0:T(128)S(1)} %get-tuple-element.78, f32[48,128,128]{2,1,0:T(8,128)} %copy.87), kind=kCustom, calls=%fused_computation.16 | custom fusion | bytes 9437376 | tf_op jit(solution)/shard_map/scatter | solution.py:55
  542.4 5.4 gather_fusion.9
  547.8 49.7 %all-reduce.11.cloned.1.call-done = f32[48,128,128]{2,0,1:T(8,128)} async-done(((f32[48,128,128]{2,0,1:T(8,128)}), f32[48,128,128]{2,0,1:T(8,128)}) %all-reduce.11.cloned.1.call-update) | async-done | bytes 3145744 | tf_op jit(solution)/shard_map/psum | solution.py:51
  609.6 9.2 %scatter_fusion.3 = f32[96,128,128]{2,1,0:T(8,128)} fusion(f32[96,128,128]{2,1,0:T(8,128)} %scatter_fusion.2, s32[48]{0:T(128)S(1)} %get-tuple-element.62, f32[48,128,128]{2,1,0:T(8,128)} %copy.95), kind=kCustom, calls=%fused_computation.17 | custom fusion | bytes 9437376 | tf_op jit(solution)/shard_map/scatter | solution.py:55
  639.3 21.5 %psum.63 = f32[96,128]{1,0:T(8,128)S(1)} all-reduce(f32[96,128]{1,0:T(8,128)S(1)} %multiply_reduce_fusion), channel_id=1, replica_groups=mesh['pix'=8,'tm'=4] {'tm'}, use_global_device_ids=true, to_apply=%region_20.24 | all-reduce | flops 12288 | bytes 98304 | tf_op jit(solution)/shard_map/psum | solution.py:58
  661.5 16.7 %reduce-scatter.9.cloned.1.call-done = f32[4,256,128]{2,1,0:T(8,128)} async-done(((f32[16,256,128]{2,1,0:T(8,128)}), f32[4,256,128]{2,1,0:T(8,128)}) %reduce-scatter.9.cloned.1.call-update) | async-done | bytes 524304 | tf_op jit(solution)/shard_map/reduce_scatter | solution.py:62
  684.6 40.6 %all-gather.9.cloned.1.call-done = f32[16,256,128]{2,1,0:T(8,128)} async-done(((f32[4,256,128]{2,1,0:T(8,128)}), f32[16,256,128]{2,1,0:T(8,128)}) %all-gather.9.cloned.1.call-update) | async-done | bytes 2097168 | tf_op jit(solution)/shard_map/all_gather | solution.py:72
  740.6 38.4 %reduce-scatter.11.cloned.1.call-done = f32[4,256,128]{2,1,0:T(8,128)} async-done(((f32[16,256,128]{2,1,0:T(8,128)}), f32[4,256,128]{2,1,0:T(8,128)}) %reduce-scatter.11.cloned.1.call-update) | async-done | bytes 524304 | tf_op jit(solution)/shard_map/reduce_scatter | solution.py:62
  780.9 45.0 %all-gather.11.cloned.1.call-done = f32[16,256,128]{2,1,0:T(8,128)} async-done(((f32[4,256,128]{2,1,0:T(8,128)}), f32[16,256,128]{2,1,0:T(8,128)}) %all-gather.11.cloned.1.call-update) | async-done | bytes 2097168 | tf_op jit(solution)/shard_map/all_gather | solution.py:72
  (185 shorter events, 225.7 us)
Async XLA Ops:
  7.2 6.5 copy-start.27
  7.2 6.4 copy-start.29
  7.2 6.4 copy-start.28
  7.2 100.4 %all-reduce.5.cloned.1.call-start = ((), (), s32[]{:S(2)}) async-start(), calls=%async_computation.4 | async-start | bytes 6291456 | tf_op jit(solution)/shard_map/psum | solution.py:51
  34.4 164.8 %all-reduce.7.cloned.1.call-start = ((), (), s32[]{:S(2)}) async-start(), calls=%async_computation.5 | async-start | bytes 6291456 | tf_op jit(solution)/shard_map/psum | solution.py:51
  107.6 5.3 copy-start.10
  129.8 145.8 %reduce-scatter.5.cloned.1.call-start = ((), (), s32[]{:S(2)}) async-start(), calls=%async_computation.6 | async-start | bytes 2621440 | tf_op jit(solution)/shard_map/reduce_scatter | solution.py:62
  230.2 92.5 %all-gather.5.cloned.1.call-start = ((), (), s32[]{:S(2)}) async-start(), calls=%async_computation.7 | async-start | bytes 2621440 | tf_op jit(solution)/shard_map/all_gather | solution.py:72
  277.7 98.5 %reduce-scatter.7.cloned.1.call-start = ((), (), s32[]{:S(2)}) async-start(), calls=%async_computation.8 | async-start | bytes 2621440 | tf_op jit(solution)/shard_map/reduce_scatter | solution.py:62
  322.7 5.8 copy-start.23
  333.6 89.7 %all-gather.7.cloned.1.call-start = ((), (), s32[]{:S(2)}) async-start(), calls=%async_computation.9 | async-start | bytes 2621440 | tf_op jit(solution)/shard_map/all_gather | solution.py:72
  333.7 6.1 copy-start.25
  347.6 78.6 %copy-start.12 = (f32[16,256,128]{1,2,0:T(8,128)S(1)}, f32[16,256,128]{1,2,0:T(8,128)}, u32[]{:S(2)}) copy-start(f32[16,256,128]{1,2,0:T(8,128)} %copy-done.11) | copy-start | bytes 6291460
  347.6 78.6 %copy-start.24 = (f32[16,128,128]{2,1,0:T(8,128)S(1)}, f32[16,128,128]{2,1,0:T(8,128)}, u32[]{:S(2)}) copy-start(f32[16,128,128]{2,1,0:T(8,128)} %gather_fusion.6) | copy-start | bytes 3145732
  378.3 129.5 %all-reduce.9.cloned.1.call-start = ((), (), s32[]{:S(2)}) async-start(), calls=%async_computation.10 | async-start | bytes 6291456 | tf_op jit(solution)/shard_map/psum | solution.py:51
  426.2 4.6 copy-start.18
  438.7 5.4 copy-start.6
  438.7 158.8 %all-reduce.11.cloned.1.call-start = ((), (), s32[]{:S(2)}) async-start(), calls=%async_computation.11 | async-start | bytes 6291456 | tf_op jit(solution)/shard_map/psum | solution.py:51
  507.7 5.6 copy-start.7
  528.0 150.2 %reduce-scatter.9.cloned.1.call-start = ((), (), s32[]{:S(2)}) async-start(), calls=%async_computation.12 | async-start | bytes 2621440 | tf_op jit(solution)/shard_map/reduce_scatter | solution.py:62
  597.5 5.4 copy-start.9
  632.8 92.4 %all-gather.9.cloned.1.call-start = ((), (), s32[]{:S(2)}) async-start(), calls=%async_computation.13 | async-start | bytes 2621440 | tf_op jit(solution)/shard_map/all_gather | solution.py:72
  680.2 98.8 %reduce-scatter.11.cloned.1.call-start = ((), (), s32[]{:S(2)}) async-start(), calls=%async_computation.14 | async-start | bytes 2621440 | tf_op jit(solution)/shard_map/reduce_scatter | solution.py:62
  736.4 89.5 %all-gather.11.cloned.1.call-start = ((), (), s32[]{:S(2)}) async-start(), calls=%async_computation.15 | async-start | bytes 2621440 | tf_op jit(solution)/shard_map/all_gather | solution.py:72
  (18 other events, 53.0 us)
Sparse Core Ops, SparseCore 0:
  34.6 72.9 all-reduce.4
  129.9 69.3 all-reduce.6
  230.3 45.2 reduce-scatter.4
  277.8 44.8 all-gather.4
  333.7 42.4 reduce-scatter.6
  378.4 44.8 all-gather.6
  438.8 68.8 all-reduce.8
  528.1 69.3 all-reduce.10
  632.9 45.2 reduce-scatter.8
  680.3 44.8 all-gather.8
  736.5 42.4 reduce-scatter.10
  781.0 44.8 all-gather.10
where the time goes:
time: 851 us; the launch traced here: 842 us
  waiting for transfers between devices  446 us (52%)
  local copies, waits for them, and re-layouts  151 us (18%)
  blocking collectives  95.3 us (11%)
  matrix products  90.3 us (11%)
  other arithmetic  42.4 us (5%)
  between operations  15.2 us (2%)
    psum x4, waiting for transfers between devices, local(): totals = lax.psum(partial_totals, 'pix')  176 us
    all_gather x4, waiting for transfers between devices, local(): updated = lax.all_gather(new_patches, 'tm', axis=0, tiled=True)  171 us
    reduce_scatter x4, waiting for transfers between devices, local(): lax.psum_scatter(partial_weights, 'tm', scatter_dimension=0, tiled=True)  98.7 us
    dot_general x29, matrix products, product(): return jnp.einsum(form, left, right, precision=lax.Precision.HIGHEST)  90.3 us
    psum x2, blocking collectives, local(): norms = lax.psum(partial_norms, 'pix')  52.4 us
    psum x2, blocking collectives, local(): energy = lax.psum(jnp.sum(traces * traces, axis=2), 'tm')  42.9 us
    scatter x4, local copies, waits for them, and re-layouts, local(): traces = traces.at[chosen].set(after)  36.6 us
    unnamed x65, local copies, waits for them, and re-layouts  31.8 us
  transfers between devices with their start and end apart: 12, of which 12 were waited for; matrix products, arithmetic and copies ran while one was open for 11% of the time, Pallas kernels for 0%

commit v1 on v0

v1 whole, which is shorter than its diff:
```python
import functools

import jax
import jax.numpy as jnp
from jax import lax
from jax.experimental import pallas as pl
from jax.experimental.pallas import tpu as pltpu
from jax.sharding import PartitionSpec as P


EPSILON = 1e-06
SUBLANES = 8
f32 = jnp.float32
bf16 = jnp.bfloat16


def up8(n):
    return -(-n // SUBLANES) * SUBLANES


def divisor(n, limits):
    return max(m for m in limits if n % m == 0)


def split(x):
    high = x.astype(bf16)
    return high, (x - high.astype(f32)).astype(bf16)


def dot(a, b, ca, cb):
    return lax.dot_general(a, b, (((ca,), (cb,)), ((), ())), preferred_element_type=f32)


def rows_by_rows(a, b):
    left = jnp.concatenate(a, axis=1)
    right = jnp.concatenate([b[0], b[0]], axis=1)
    return dot(left, right, 1, 1) + dot(a[0], b[1], 1, 1)


def rows_by_columns(a, b, ca=1):
    n = b[0].shape[1]
    both = dot(a[0], jnp.concatenate(b, axis=1), ca, 0)
    return both[:, :n] + both[:, n:] + dot(a[1], b[0], ca, 0)


def full_spec(shape):
    return pl.BlockSpec(shape, lambda *_: (0,) * len(shape))


def squares(x):
    return jnp.sum(x * x, axis=0, keepdims=True)


def first_kernel(bl, y, foot, *refs, parts, own, step):
    t0s, t1s = refs[:step], refs[step:2 * step]
    pos, base_out, pay = refs[2 * step:]
    at = pl.program_id(0) * step
    count = pl.num_programs(0) * step
    kb = foot.shape[3]
    for i in range(step):
        f0, f1 = split(foot[i, 0]), split(foot[i, 1])
        base = y[i].astype(f32) - rows_by_columns(f1, split(t1s[i][0]))
        base_out[i] = base
        residual = base - rows_by_columns(f0, split(t0s[i][0]))
        terms = rows_by_columns(split(residual), f0, 0)
        p = at + i
        pay[:, pl.ds(pl.multiple_of(p * own, SUBLANES), own), :] = terms.reshape(parts, own, kb)
        for g in range(2):
            norm = jnp.broadcast_to(squares(foot[i, g])[None], (parts, 1, kb))
            pay[:, pl.ds(count * own + g * count + p, 1), :] = norm

    @pl.when(at == 0)
    def _():
        start = pay.shape[1] - pos.shape[0]
        pay[:, start:, :] = jnp.broadcast_to(pos[...][None], (parts,) + pos.shape)


def second_kernel(base, foot, rx, pay, *, parts, own, step):
    at = pl.program_id(0) * step
    kb = foot.shape[3]
    for i in range(step):
        f0, f1 = split(foot[i, 0]), split(foot[i, 1])
        trace = rx[:, i].reshape(parts * own, kb)
        residual = base[i] - rows_by_rows(f0, split(trace))
        terms = rows_by_columns(split(residual), f1, 0)
        pay[:, pl.ds(pl.multiple_of((at + i) * own, SUBLANES), own), :] = terms.reshape(parts, own, kb)


def prepare_kernel(order, pix, *refs, own, step):
    ins, out, flipped = refs[:step], refs[step], refs[step + 1]
    for i in range(step):
        flipped[i] = ins[i][0].T
        out[i] = flipped[i, pl.ds(pl.multiple_of(pix[0] * own, SUBLANES), own), :]


def owner_kernel(listing, place, order, rx, before, *refs, group, per, own, outs, outper, other):
    if other == "norms":
        after, back, norms1, totals, norms = refs
        norms1[...] = jnp.zeros(norms1.shape, f32)
        norms[...] = jnp.zeros(norms.shape, f32)
    elif other == "final":
        norms, after0, after, back, final, totals = refs
    else:
        norms, after, back, totals = refs
    sources = rx.shape[0]
    kb = rx.shape[2]
    bpg = before.shape[0]
    totals[...] = jnp.zeros(totals.shape, f32)

    @pl.loop(0, sources)
    def _(s):
        for i in range(per):
            p = s * per + i
            j = place[listing[p, group]] - group * bpg
            totals[j] = totals[j] + rx[s, i * own:(i + 1) * own, :]
            if other == "norms":
                row = per * own + i
                norms[j] = norms[j] + jnp.broadcast_to(rx[s, row:row + 1, :], (SUBLANES, kb))
                j1 = place[listing[p, 1]] - bpg
                row = per * own + per + i
                norms1[j1] = norms1[j1] + jnp.broadcast_to(rx[s, row:row + 1, :], (SUBLANES, kb))

    scale = kb * norms[:, 0:1, :] + EPSILON
    after[...] = jnp.maximum(before[...] + totals[...] / scale, 0.0)

    @pl.loop(0, outs)
    def _(s):
        for i in range(outper):
            j = place[listing[s * outper + i, group]] - group * bpg
            back[s, i * own:(i + 1) * own, :] = after[j]

    if other == "final":

        @pl.loop(0, bpg, unroll=4)
        def _(j):
            final[order[j]] = after0[j]
            final[order[bpg + j]] = after[j]


def owner(tables, rx, before, extra, *, group, per, outs, outper, other):
    bpg, own, kb = before.shape
    norms_shape = (bpg, SUBLANES, kb)
    shapes = [before.shape, (outs, outper * own, kb)]
    if other == "norms":
        shapes.append(norms_shape)
    if other == "final":
        shapes.append((2 * bpg, own, kb))
    scratch = [pltpu.VMEM(before.shape, f32)]
    if other == "norms":
        scratch.append(pltpu.VMEM(norms_shape, f32))
    return pl.pallas_call(
        functools.partial(owner_kernel, group=group, per=per, own=own, outs=outs, outper=outper, other=other),
        grid_spec=pltpu.PrefetchScalarGridSpec(
            num_scalar_prefetch=3,
            grid=(1,),
            in_specs=[full_spec(x.shape) for x in (rx, before, *extra)],
            out_specs=[full_spec(shape) for shape in shapes],
            scratch_shapes=scratch,
        ),
        out_shape=[jax.ShapeDtypeStruct(shape, f32) for shape in shapes],
        name="owner",
    )(*tables, rx, before, *extra)


def incoming(rx, i, me, ntm):
    pieces = []
    for s in range(ntm):
        piece = rx[:, lax.rem(me + (ntm - s), ntm), i]
        pieces.append(piece.reshape(piece.shape[0] * piece.shape[1], piece.shape[2]))
    return jnp.concatenate(pieces, axis=0)


def outgoing(pay, terms, p, me, ntm):
    npix, kb = pay.shape[0], terms.shape[1]
    own = terms.shape[0] // (npix * ntm)
    for s in range(ntm):
        piece = terms[s * npix * own:(s + 1) * npix * own].reshape(npix, own, kb)
        to = lax.rem(me + (ntm - s), ntm)
        pay[:, to, pl.ds(pl.multiple_of(p * own, SUBLANES), own), :] = piece


def footprint_phase(residual, f0, f1, t0, t1):
    kb = f0.shape[1]
    scale0 = kb * squares(t0) + EPSILON
    scale1 = kb * squares(t1) + EPSILON
    s0, s1 = split(t0), split(t1)
    n0 = jnp.maximum(f0 + rows_by_columns(split(residual), s0) / scale0, 0.0)
    residual = residual - rows_by_rows(split(n0 - f0), s0)
    n1 = jnp.maximum(f1 + rows_by_columns(split(residual), s1) / scale1, 0.0)
    return residual, n0, n1, s1


def merge_kernel(me_ref, *refs, ntm, step):
    ys, t0s = refs[:ntm], refs[ntm:2 * ntm]
    foot, residual_out, t0_out = refs[2 * ntm:]
    kb = foot.shape[3]
    for i in range(step):
        y = jnp.concatenate([ref[i] for ref in ys], axis=1)
        t0 = jnp.concatenate([ref[:, i].reshape(ref.shape[0] * ref.shape[2], kb) for ref in t0s], axis=0)
        residual_out[i] = y - rows_by_rows(split(foot[i, 0]), split(t0))
        t0_out[i] = t0


def third_kernel(me_ref, part, t0_in, rx1, foot, residual_out, foot_out, t1_out, pay, *, ntm, step):
    me = me_ref[0]
    at = pl.program_id(0) * step
    count = pl.num_programs(0) * step
    for i in range(step):
        f0, f1 = foot[i, 0], foot[i, 1]
        t1 = incoming(rx1, i, me, ntm)
        residual = part[i] - rows_by_rows(split(f1), split(t1))
        residual, n0, n1, s1 = footprint_phase(residual, f0, f1, t0_in[i], t1)
        residual = residual - rows_by_rows(split(n1 - f1), s1)
        residual_out[i] = residual
        foot_out[i, 0] = n0
        foot_out[i, 1] = n1
        t1_out[i] = t1
        outgoing(pay, rows_by_columns(split(residual), split(n0), 0), at + i, me, ntm)
        own = (pay.shape[2] - up8(2 * count)) // count
        for g, new in enumerate((n0, n1)):
            norm = jnp.broadcast_to(squares(new)[None, None], pay.shape[:2] + (1, new.shape[1]))
            pay[:, :, pl.ds(count * own + g * count + at + i, 1), :] = norm


def ahead_kernel(residual, foot, terms_out, gram_out, *, step):
    for i in range(step):
        f1 = split(foot[i, 1])
        terms_out[i] = rows_by_columns(split(residual[i]), f1, 0)
        gram_out[i] = rows_by_columns(split(foot[i, 0]), f1, 0)


def fourth_kernel(me_ref, terms, gram, told, rx, change_out, pay, *, ntm, step):
    me = me_ref[0]
    at = pl.program_id(0) * step
    for i in range(step):
        change = incoming(rx, i, me, ntm) - told[i]
        change_out[i] = change
        new = terms[i] - rows_by_columns(split(change), split(gram[i]))
        outgoing(pay, new, at + i, me, ntm)


def late_kernel(residual, foot, change, residual_out, *, step):
    for i in range(step):
        residual_out[i] = residual[i] - rows_by_rows(split(foot[i, 0]), split(change[i]))


def last_kernel(me_ref, residual_in, foot, told, rx0, rx1, foot_out, *, ntm, step):
    me = me_ref[0]
    for i in range(step):
        f0, f1 = foot[i, 0], foot[i, 1]
        t0 = incoming(rx0, i, me, ntm)
        t1 = incoming(rx1, i, me, ntm)
        residual = residual_in[i] - rows_by_rows(split(f1), split(t1 - told[i]))
        _, n0, n1, _ = footprint_phase(residual, f0, f1, t0, t1)
        foot_out[i, 0] = n0
        foot_out[i, 1] = n1


def flip_kernel(rx, out):
    npix, count, own, kb = rx.shape
    for j in range(count):
        out[j] = rx[:, j].reshape(npix * own, kb).T


def line_gather(chunks, axis, n):
    me = lax.axis_index(axis)
    size = sum(x.shape[0] for x in chunks)
    rest = chunks[0].shape[1:]
    left, right = list(chunks), list(chunks)
    from_left, from_right = {}, {}
    for s in range(1, n):
        for c in range(len(chunks)):
            left[c] = lax.ppermute(left[c], axis, [(j, j + 1) for j in range(n - 1)])
            right[c] = lax.ppermute(right[c], axis, [(j, j - 1) for j in range(1, n)])
            from_left[s, c], from_right[s, c] = left[c], right[c]
    out = jnp.zeros((n * size,) + rest, chunks[0].dtype)
    offset = 0
    for c, x in enumerate(chunks):
        out = lax.dynamic_update_slice_in_dim(out, x, me * size + offset, 0)
        for s in range(1, n):
            piece = jnp.where(me + s < n, from_right[s, c], from_left[n - s, c])
            out = lax.dynamic_update_slice_in_dim(out, piece, lax.rem(me + s, n) * size + offset, 0)
        offset += x.shape[0]
    return out


def local(recording, footprints, traces, block_list, block_order, *, npix, ntm):
    count, voxels, frames = recording.shape
    groups, kb = footprints.shape[1], footprints.shape[3]
    blocks = traces.shape[0]
    bpg = blocks // groups
    own = frames // npix
    share = count // ntm
    everyone = npix * ntm
    every = frames * ntm
    pix, tm = lax.axis_index("pix"), lax.axis_index("tm")
    me = jnp.reshape(tm, (1,)).astype(jnp.int32)

    def kernel(body, grid, in_specs, out_specs, out_shape, prefetch=0, scratch=(), **static):
        return pl.pallas_call(
            functools.partial(body, **static),
            grid_spec=pltpu.PrefetchScalarGridSpec(
                num_scalar_prefetch=prefetch,
                grid=grid,
                in_specs=in_specs,
                out_specs=out_specs,
                scratch_shapes=scratch,
            ),
            out_shape=out_shape,
        )

    def array(*shape):
        return jax.ShapeDtypeStruct(shape, f32)

    def exchange(x, axes):
        return lax.all_to_all(x, axes, 0, 0, tiled=True)

    y_pieces = []
    for s in range(ntm):
        to = lax.rem(tm + s, ntm)
        piece = lax.dynamic_slice_in_dim(recording, to * share, share, 0).astype(f32)
        y_pieces.append(lax.ppermute(piece, "tm", [(j, (j + s) % ntm) for j in range(ntm)]) if s else piece)

    pos_rows = up8(-(-count * groups // kb))
    pos_row = jnp.pad(
        block_list.astype(f32).reshape(-1), (0, pos_rows * kb - count * groups)
    ).reshape(pos_rows, kb)
    place = jnp.zeros((blocks,), jnp.int32).at[block_order].set(jnp.arange(blocks, dtype=jnp.int32))

    step = divisor(count, (4, 2, 1))
    rows = count * own + up8(groups * count)
    foot_spec = pl.BlockSpec((step, groups, voxels, kb), lambda p, *_: (p, 0, 0, 0))
    patch_spec = pl.BlockSpec((step, voxels, frames), lambda p, *_: (p, 0, 0))

    def block_spec(i, g):
        return pl.BlockSpec((1, kb, frames), lambda p, bl: (bl[p * step + i, g], 0, 0))

    base, pay = kernel(
        first_kernel, (count // step,),
        [patch_spec, foot_spec] + [block_spec(i, g) for g in range(groups) for i in range(step)]
        + [full_spec(pos_row.shape)],
        [patch_spec, full_spec((npix, rows + pos_rows, kb))],
        [array(count, voxels, frames), array(npix, rows + pos_rows, kb)],
        prefetch=1, parts=npix, own=own, step=step,
    )(block_list, recording, footprints, *[traces] * (groups * step), pos_row)
    got = exchange(pay, "pix")

    several = divisor(bpg, (8, 4, 2, 1))
    whereabouts = jnp.reshape(pix, (1,)).astype(jnp.int32)

    def prepared(g):
        def ordered_spec(i):
            return pl.BlockSpec(
                (1, kb, frames), lambda b, order, pix: (order[g * bpg + b * several + i], 0, 0)
            )

        return kernel(
            prepare_kernel, (bpg // several,),
            [ordered_spec(i) for i in range(several)],
            pl.BlockSpec((several, own, kb), lambda b, *_: (b, 0, 0)),
            array(bpg, own, kb),
            prefetch=2, scratch=[pltpu.VMEM((several, frames, kb), f32)], own=own, step=several,
        )(block_order, whereabouts, *[traces] * several)

    before0, before1 = prepared(0), prepared(1)

    listing = got[:, rows:, :].reshape(npix, -1)[:, :count * groups].reshape(npix * count, groups)
    tables = (listing.astype(jnp.int32), place, block_order)
    after0, back, norms1 = owner(
        tables, got, before0, (), group=0, per=count, outs=npix, outper=count, other="norms"
    )
    rx0 = exchange(back, "pix").reshape(npix, count, own, kb)

    t0_pieces = []
    for s in range(ntm):
        to = lax.rem(tm + s, ntm)
        piece = lax.dynamic_slice_in_dim(rx0, to * share, share, 1)
        t0_pieces.append(lax.ppermute(piece, "tm", [(j, (j + s) % ntm) for j in range(ntm)]) if s else piece)

    pay = kernel(
        second_kernel, (count // step,),
        [patch_spec, foot_spec, pl.BlockSpec((npix, step, own, kb), lambda p: (0, p, 0, 0))],
        full_spec((npix, count * own, kb)),
        array(npix, count * own, kb),
        parts=npix, own=own, step=step,
    )(base, footprints, rx0)
    after1, back = owner(
        tables, exchange(pay, "pix"), before1, (norms1,),
        group=1, per=count, outs=everyone, outper=share, other=None,
    )

    def spread(x):
        return exchange(x.reshape(everyone, x.shape[-2], kb), ("pix", "tm"))

    def landed(x):
        return x.reshape(npix, ntm, share, own, kb)

    rx1 = landed(spread(back))

    step = divisor(share, (2, 1))
    grid = (share // step,)
    share_spec = pl.BlockSpec((step, voxels, frames), lambda p, *_: (p, 0, 0))
    part_spec = pl.BlockSpec((npix, step, own, kb), lambda p, *_: (0, p, 0, 0))
    rx_spec = pl.BlockSpec((npix, ntm, step, own, kb), lambda p, *_: (0, 0, p, 0, 0))
    residual_spec = pl.BlockSpec((step, voxels, every), lambda p, *_: (p, 0, 0))
    trace_spec = pl.BlockSpec((step, every, kb), lambda p, *_: (p, 0, 0))
    gram_spec = pl.BlockSpec((step, kb, kb), lambda p, *_: (p, 0, 0))
    foot_spec = pl.BlockSpec((step, groups, voxels, kb), lambda p, *_: (p, 0, 0, 0))
    own_foot_spec = pl.BlockSpec(
        (step, groups, voxels, kb), lambda p, me: (me[0] * (share // step) + p, 0, 0, 0)
    )
    residual_type, trace_type = array(share, voxels, every), array(share, every, kb)
    foot_type = array(share, groups, voxels, kb)
    wide = (npix, ntm, share * own + up8(groups * share), kb)
    narrow = (npix, ntm, share * own, kb)

    part, t0_old = kernel(
        merge_kernel, grid,
        [share_spec] * ntm + [part_spec] * ntm + [own_foot_spec],
        [residual_spec, trace_spec],
        [residual_type, trace_type],
        prefetch=1, ntm=ntm, step=step,
    )(me, *y_pieces, *t0_pieces, footprints)
    residual, foot, t1_old, pay = kernel(
        third_kernel, grid,
        [residual_spec, trace_spec, rx_spec, own_foot_spec],
        [residual_spec, foot_spec, trace_spec, full_spec(wide)],
        [residual_type, foot_type, trace_type, array(*wide)],
        prefetch=1, ntm=ntm, step=step,
    )(me, part, t0_old, rx1, footprints)

    got = spread(pay)
    terms, gram = kernel(
        ahead_kernel, grid,
        [residual_spec, foot_spec],
        [trace_spec, gram_spec],
        [trace_type, array(share, kb, kb)],
        step=step,
    )(residual, foot)
    after0, back, norms1 = owner(
        tables, got, after0, (), group=0, per=share, outs=everyone, outper=share, other="norms"
    )
    rx0 = landed(spread(back))
    change, pay = kernel(
        fourth_kernel, grid,
        [trace_spec, gram_spec, trace_spec, rx_spec],
        [trace_spec, full_spec(narrow)],
        [trace_type, array(*narrow)],
        prefetch=1, ntm=ntm, step=step,
    )(me, terms, gram, t0_old, rx0)
    got = spread(pay)
    residual = kernel(
        late_kernel, grid,
        [residual_spec, foot_spec, trace_spec],
        residual_spec,
        residual_type,
        step=step,
    )(residual, foot, change)
    after1, back, final = owner(
        tables, got, after1, (norms1, after0), group=1, per=share, outs=everyone, outper=share, other="final"
    )
    rx1 = landed(spread(back))

    halves = divisor(share, (2, 1))
    half = share // halves
    chunks = []
    for c in range(halves):
        step = divisor(half, (2, 1))
        skip = c * half // step

        def at(spec, axis):
            shape, index = spec

            def moved(p, me, index=index, skip=skip, axis=axis):
                return tuple(skip + p if a == axis else 0 for a in range(index))

            return pl.BlockSpec(shape, moved)

        chunks.append(
            kernel(
                last_kernel, (half // step,),
                [
                    at(((step, voxels, every), 3), 0),
                    at(((step, groups, voxels, kb), 4), 0),
                    at(((step, every, kb), 3), 0),
                    at(((npix, ntm, step, own, kb), 5), 2),
                    at(((npix, ntm, step, own, kb), 5), 2),
                ],
                pl.BlockSpec((step, groups, voxels, kb), lambda p, *_: (p, 0, 0, 0)),
                array(half, groups, voxels, kb),
                prefetch=1, ntm=ntm, step=step,
            )(me, residual, foot, t1_old, rx0, rx1)
        )
    footprints_out = line_gather(chunks, "tm", ntm)

    gathered = lax.all_gather(final, "pix", axis=0)
    traces_out = kernel(
        flip_kernel, (blocks // several,),
        [pl.BlockSpec((npix, several, own, kb), lambda j: (0, j, 0, 0))],
        pl.BlockSpec((several, kb, frames), lambda j: (j, 0, 0)),
        array(blocks, kb, frames),
    )(gathered)
    return footprints_out, traces_out


def solution(mesh):
    npix, ntm = mesh.shape["pix"], mesh.shape["tm"]
    in_specs = (
        P("pix", None, "tm"),
        P("pix", None, None, None),
        P(None, None, "tm"),
        P("pix", None),
        P(),
    )
    out_specs = (P("pix", None, None, None), P(None, None, "tm"))

    def body(*args):
        return local(*args, npix=npix, ntm=ntm)

    return jax.shard_map(body, mesh=mesh, in_specs=in_specs, out_specs=out_specs, check_vma=False)
```

time: 851 us -> 452 us (0.53)
  waiting for transfers between devices: 446 us -> 164 us
  local copies, waits for them, and re-layouts: 151 us -> 15 us
  Pallas kernels: 0 us -> 94.8 us
  matrix products: 90.3 us -> 0 us
  starting transfers between devices: 1.48 us -> 63.9 us
  other arithmetic: 42.4 us -> 8.94 us
    psum x4 -> x0, waiting for transfers between devices: 176 us -> none  [local(): totals = lax.psum(partial_totals, 'pix')]
    all_gather x4 -> x1, waiting for transfers between devices: 171 us -> 0.01 us  [local(): gathered = lax.all_gather(final, 'pix', axis=0)]
    ppermute x0 -> x18, waiting for transfers between devices: none -> 102 us  [the longest x6 78.8 us: local(): lax.ppermute(piece, 'tm', [(j, (j + s) % ntm) for j in range(ntm)])]
    reduce_scatter x4 -> x0, waiting for transfers between devices: 98.7 us -> none  [local(): lax.psum_scatter(partial_weights, 'tm', scatter_dimension=0, tiled=True)]
    psum x4 -> x0, blocking collectives: 95.3 us -> none  [the longest x2 52.4 us: local(): norms = lax.psum(partial_norms, 'pix')]
    pallas_call x0 -> x16, Pallas kernels: none -> 94.8 us  [the longest x4 22.4 us: owner(): pl.pallas_call(functools.partial(owner_kernel, group=group, per=per, own=...]
    dot_general x29 -> x0, matrix products: 90.3 us -> none  [product(): return jnp.einsum(form, left, right, precision=lax.Precision.HIGHEST)]
    all_to_all x0 -> x3, blocking collectives: none -> 88.1 us  [exchange(): return lax.all_to_all(x, axes, 0, 0, tiled=True)]
  transfers between devices with their start and end apart: 12 -> 24, of which waited for: 12 -> 15; matrix products, arithmetic and copies ran while one was open for 11% -> 3% of each run, Pallas kernels for 0% -> 7%
where the time goes in v1:
time: 452 us; the launch traced here: 449 us
  waiting for transfers between devices  164 us (36%)
  Pallas kernels  94.8 us (21%)
  blocking collectives  88.1 us (19%)
  starting transfers between devices  63.9 us (14%)
  local copies, waits for them, and re-layouts  15 us (3%)
  between operations  14.3 us (3%)
  other arithmetic  8.94 us (2%)
    all_to_all x3, blocking collectives, exchange(): return lax.all_to_all(x, axes, 0, 0, tiled=True)  88.1 us
    ppermute x6, waiting for transfers between devices, local(): lax.ppermute(piece, 'tm', [(j, (j + s) % ntm) for j in range(ntm)])  78.8 us
    all_to_all x5, waiting for transfers between devices, exchange(): return lax.all_to_all(x, axes, 0, 0, tiled=True)  62 us
    ppermute x6, starting transfers between devices, line_gather(): left[c] = lax.ppermute(left[c], axis, [(j, j + 1) for j in range(n - 1)])  28.9 us
    pallas_call x4, Pallas kernels, owner(): pl.pallas_call(functools.partial(owner_kernel, group=group, per=per, own=...  22.4 us
    ppermute x6, waiting for transfers between devices, line_gather(): left[c] = lax.ppermute(left[c], axis, [(j, j + 1) for j in range(n - 1)])  20.4 us
    all_to_all x5, starting transfers between devices, exchange(): return lax.all_to_all(x, axes, 0, 0, tiled=True)  20.1 us
    pallas_call x2, Pallas kernels, prepared(): kernel(prepare_kernel, (bpg // several,), [ordered_spec(i) for i in range...  11.6 us
  transfers between devices with their start and end apart: 24, of which 15 were waited for; matrix products, arithmetic and copies ran while one was open for 3% of the time, Pallas kernels for 7%

profile of v1, /device:TPU:0, one launch (start us, length us, event | category | flops | bytes accessed | tf_op | source)
XLA Modules:
  0.0 449.3 jit_solution(15618645858345185715)
XLA Ops:
  10.0 10.3 %shard_map.68 = (f32[16,256,128]{2,1,0:T(8,128)}, f32[8,296,128]{2,1,0:T(8,128)}) custom-call(s32[16,2]{1,0:T(8,128)} %copy.12.bl, bf16[16,256,128]{2,1,0:T(8,128)(2,1)} %y.3, f32[16,2,256,128]{3,2,1,0:T(8,128)} %foot.5, f32[96,128,128]{2,1,0:T(8,128)} %refs_7_.5, f32[96,128,128]{2,1,0:T(8,128)} %refs_7_.5, f32[96,128,128]{2,1,0:T(8,128)} %refs_7_.5, ...), custom_call_target="tpu_custom_call" | custom-call | tf_op jit(solution)/shard_map/pallas_call | solution.py:338
  25.4 5.8 %shard_map.69.before = f32[48,16,128]{2,1,0:T(8,128)} custom-call(s32[96]{0:T(128)} %order.11, s32[1]{0:T(128)} %bitcast.2.pix, f32[96,128,128]{2,1,0:T(8,128)} %refs_7_.5, f32[96,128,128]{2,1,0:T(8,128)} %refs_7_.5, f32[96,128,128]{2,1,0:T(8,128)} %refs_7_.5, f32[96,128,128]{2,1,0:T(8,128)} %refs_7_.5, f32[96,128,128]{2,1,0:T(8,128)} %refs_7_.5, ...), custom_call_target="tpu_custom_call" | custom-call | tf_op jit(solution)/shard_map/pallas_call | solution.py:357
  32.6 9.9 %all-to-all-done.rx = f32[8,296,128]{2,1,0:T(8,128)S(1)} async-done(((f32[8,296,128]{2,1,0:T(8,128)}), f32[8,296,128]{2,1,0:T(8,128)S(1)}, u32[]{:S(2)}, u32[]{:S(2)}) %all-to-all-start) | async-done | bytes 1212448 | tf_op jit(solution)/shard_map/all_to_all | solution.py:316
  43.6 5.3 %owner.4 = (f32[48,16,128]{2,1,0:T(8,128)}, f32[8,256,128]{2,1,0:T(8,128)}, f32[48,8,128]{2,1,0:T(8,128)}) custom-call(s32[128,2]{1,0:T(8,128)} %convert_element_type.28.listing, s32[96]{0:T(128)} %scatter_custom_fusion.place, s32[96]{0:T(128)} %order.11, f32[8,296,128]{2,1,0:T(8,128)} %copy-done.3, f32[48,16,128]{2,1,0:T(8,128)} %shard_map.69.before), custom_call_target="tpu_custom_call" | custom-call | tf_op jit(solution)/shard_map/owner/pallas_call | solution.py:151
  48.9 19.6 %all_to_all.40 = f32[8,256,128]{2,1,0:T(8,128)} all-to-all(f32[8,256,128]{2,1,0:T(8,128)} %get-tuple-element.25), channel_id=1, replica_groups=mesh['pix'=8,'tm'=4] {'pix'}, dimensions={0} | all-to-all | bytes 2097152 | tf_op jit(solution)/shard_map/all_to_all | solution.py:316
  68.5 7.9 %shard_map.71 = f32[8,256,128]{2,1,0:T(8,128)} custom-call(f32[16,256,128]{2,1,0:T(8,128)} %get-tuple-element.28.base, f32[16,2,256,128]{3,2,1,0:T(8,128)} %foot.5, f32[8,16,16,128]{3,2,1,0:T(8,128)} %bitcast.21), custom_call_target="tpu_custom_call" | custom-call | tf_op jit(solution)/shard_map/pallas_call | solution.py:380
  80.0 5.8 %shard_map.72.before = f32[48,16,128]{2,1,0:T(8,128)} custom-call(s32[96]{0:T(128)} %order.11, s32[1]{0:T(128)} %bitcast.2.pix, f32[96,128,128]{2,1,0:T(8,128)} %refs_7_.5, f32[96,128,128]{2,1,0:T(8,128)} %refs_7_.5, f32[96,128,128]{2,1,0:T(8,128)} %refs_7_.5, f32[96,128,128]{2,1,0:T(8,128)} %refs_7_.5, f32[96,128,128]{2,1,0:T(8,128)} %refs_7_.5, ...), custom_call_target="tpu_custom_call" | custom-call | tf_op jit(solution)/shard_map/pallas_call | solution.py:357
  85.8 9.5 %all-to-all-done.2.rx = f32[8,256,128]{2,1,0:T(8,128)S(1)} async-done(((f32[8,256,128]{2,1,0:T(8,128)}), f32[8,256,128]{2,1,0:T(8,128)S(1)}, u32[]{:S(2)}, u32[]{:S(2)}) %all-to-all-start.2) | async-done | bytes 1048608 | tf_op jit(solution)/shard_map/all_to_all | solution.py:316
  96.2 5.4 %owner.5 = (f32[48,16,128]{2,1,0:T(8,128)}, f32[32,64,128]{2,1,0:T(8,128)}) custom-call(s32[128,2]{1,0:T(8,128)} %convert_element_type.28.listing, s32[96]{0:T(128)} %scatter_custom_fusion.place, s32[96]{0:T(128)} %order.11, f32[8,256,128]{2,1,0:T(8,128)} %copy-done.6, f32[48,16,128]{2,1,0:T(8,128)} %shard_map.72.before, f32[48,8,128]{2,1,0:T(8,128)} %get-tuple-element.29.refs_0_), custom_call_target="tpu_custom_call" | custom-call | tf_op jit(solution)/shard_map/owner/pallas_call | solution.py:151
  114.2 24.8 %collective-permute-done.refs_1_ = f32[4,256,128]{2,1,0:T(8,128)S(1)} collective-permute-done((f32[4,256,128]{2,1,0:T(8,128)S(1)}, f32[4,256,128]{2,1,0:T(8,128)S(1)}, u32[]{:S(2)}, u32[]{:S(2)}) %collective-permute-start) | collective-permute-done | bytes 524320 | tf_op jit(solution)/shard_map/ppermute | solution.py:322
  139.3 38.0 %collective-permute-done.1.refs_2_ = f32[4,256,128]{2,1,0:T(8,128)S(1)} collective-permute-done((f32[4,256,128]{2,1,0:T(8,128)S(1)}, f32[4,256,128]{2,1,0:T(8,128)S(1)}, u32[]{:S(2)}, u32[]{:S(2)}) %collective-permute-start.1) | collective-permute-done | bytes 524320 | tf_op jit(solution)/shard_map/ppermute | solution.py:322
  178.2 16.0 %collective-permute-done.4.refs_6_ = f32[8,4,16,128]{3,2,1,0:T(8,128)S(1)} collective-permute-done((f32[8,4,16,128]{3,2,1,0:T(8,128)S(1)}, f32[8,4,16,128]{3,2,1,0:T(8,128)S(1)}, u32[]{:S(2)}, u32[]{:S(2)}) %collective-permute-start.4) | collective-permute-done | bytes 262176 | tf_op jit(solution)/shard_map/ppermute | solution.py:378
  199.6 9.1 %shard_map.73 = (f32[4,256,512]{2,1,0:T(8,128)}, f32[4,2,256,128]{3,2,1,0:T(8,128)}, f32[4,512,128]{2,1,0:T(8,128)}, f32[8,4,72,128]{3,2,1,0:T(8,128)}) custom-call(s32[1]{0:T(128)} %bitcast.me_ref, f32[4,256,512]{2,1,0:T(8,128)} %get-tuple-element.26.part, f32[4,512,128]{2,1,0:T(8,128)} %get-tuple-element.27.t0_in.told, f32[8,4,4,16,128]{4,3,2,1,0:T(8,128)} %bitcast.24, ...), custom_call_target="tpu_custom_call" | custom-call | tf_op jit(solution)/shard_map/pallas_call | solution.py:424
  208.7 39.0 %all_to_all.41.rx = f32[32,72,128]{2,1,0:T(8,128)} all-to-all(f32[32,72,128]{2,1,0:T(8,128)} %bitcast.25), channel_id=1, replica_groups=mesh['pix'=8,'tm'=4] {'pix','tm'}, dimensions={0} | all-to-all | bytes 2359296 | tf_op jit(solution)/shard_map/all_to_all | solution.py:316
  247.7 5.6 %owner.6 = (f32[48,16,128]{2,1,0:T(8,128)}, f32[32,64,128]{2,1,0:T(8,128)}, f32[48,8,128]{2,1,0:T(8,128)}) custom-call(s32[128,2]{1,0:T(8,128)} %convert_element_type.28.listing, s32[96]{0:T(128)} %scatter_custom_fusion.place, s32[96]{0:T(128)} %order.11, f32[32,72,128]{2,1,0:T(8,128)} %all_to_all.41.rx, f32[48,16,128]{2,1,0:T(8,128)} %get-tuple-element.36.before), custom_call_target="tpu_custom_call" | custom-call | tf_op jit(solution)/shard_map/owner/pallas_call | solution.py:151
  259.3 21.6 %all-to-all-done.5 = f32[32,64,128]{2,1,0:T(8,128)S(1)} async-done(((f32[32,64,128]{2,1,0:T(8,128)}), f32[32,64,128]{2,1,0:T(8,128)S(1)}, u32[]{:S(2)}, u32[]{:S(2)}) %all-to-all-start.5) | async-done | bytes 1048608 | tf_op jit(solution)/shard_map/all_to_all | solution.py:316
  285.1 29.6 %all_to_all.42.rx = f32[32,64,128]{2,1,0:T(8,128)} all-to-all(f32[32,64,128]{2,1,0:T(8,128)} %bitcast.26), channel_id=1, replica_groups=mesh['pix'=8,'tm'=4] {'pix','tm'}, dimensions={0} | all-to-all | bytes 2097152 | tf_op jit(solution)/shard_map/all_to_all | solution.py:316
  314.7 6.1 %owner.7 = (f32[48,16,128]{2,1,0:T(8,128)}, f32[32,64,128]{2,1,0:T(8,128)}, f32[96,16,128]{2,1,0:T(8,128)}) custom-call(s32[128,2]{1,0:T(8,128)} %convert_element_type.28.listing, s32[96]{0:T(128)} %scatter_custom_fusion.place, s32[96]{0:T(128)} %order.11, f32[32,64,128]{2,1,0:T(8,128)} %all_to_all.42.rx, f32[48,16,128]{2,1,0:T(8,128)} %get-tuple-element.41.before, ...), custom_call_target="tpu_custom_call" | custom-call | tf_op jit(solution)/shard_map/owner/pallas_call | solution.py:151
  329.3 21.0 %all-to-all-done.7 = f32[32,64,128]{2,1,0:T(8,128)S(1)} async-done(((f32[32,64,128]{2,1,0:T(8,128)}), f32[32,64,128]{2,1,0:T(8,128)S(1)}, u32[]{:S(2)}, u32[]{:S(2)}) %all-to-all-start.7) | async-done | bytes 1048608 | tf_op jit(solution)/shard_map/all_to_all | solution.py:316
  372.9 5.3 %collective-permute-start.8 = (f32[2,2,256,128]{3,2,1,0:T(8,128)S(1)}, f32[2,2,256,128]{3,2,1,0:T(8,128)}, u32[]{:S(2)}, u32[]{:S(2)}) collective-permute-start(f32[2,2,256,128]{3,2,1,0:T(8,128)S(1)} %collective-permute-done.7), channel_id=1, source_target_pairs={{0,1},{1,2},{2,3},{4,5},{5,6},{6,7},{8,9},{9,10},{10,11},{12,13},{... | collective-permute-start | bytes 1572872 | tf_op jit(solution)/shard_map/ppermute | solution.py:273
  389.8 5.5 %collective-permute-done.8 = f32[2,2,256,128]{3,2,1,0:T(8,128)} collective-permute-done((f32[2,2,256,128]{3,2,1,0:T(8,128)S(1)}, f32[2,2,256,128]{3,2,1,0:T(8,128)}, u32[]{:S(2)}, u32[]{:S(2)}) %collective-permute-start.8) | collective-permute-done | bytes 524320 | tf_op jit(solution)/shard_map/ppermute | solution.py:273
  395.3 5.3 %collective-permute-start.9 = (f32[2,2,256,128]{3,2,1,0:T(8,128)}, f32[2,2,256,128]{3,2,1,0:T(8,128)}, u32[]{:S(2)}, u32[]{:S(2)}) collective-permute-start(f32[2,2,256,128]{3,2,1,0:T(8,128)} %collective-permute-done.8), channel_id=1, source_target_pairs={{0,1},{1,2},{2,3},{4,5},{5,6},{6,7},{8,9},{9,10},{10,11},{12,13},{... | collective-permute-start | bytes 1572872 | tf_op jit(solution)/shard_map/ppermute | solution.py:273
  412.3 5.5 %collective-permute-done.9 = f32[2,2,256,128]{3,2,1,0:T(8,128)} collective-permute-done((f32[2,2,256,128]{3,2,1,0:T(8,128)}, f32[2,2,256,128]{3,2,1,0:T(8,128)}, u32[]{:S(2)}, u32[]{:S(2)}) %collective-permute-start.9) | collective-permute-done | bytes 524320 | tf_op jit(solution)/shard_map/ppermute | solution.py:273
  432.3 10.2 %shard_map.79 = f32[96,128,128]{2,1,0:T(8,128)} custom-call(f32[8,96,16,128]{3,2,1,0:T(8,128)} %bitcast.23), custom_call_target="tpu_custom_call" | custom-call | tf_op jit(solution)/shard_map/pallas_call | solution.py:497
  (99 shorter events, 113.0 us)
Async XLA Ops:
  20.2 22.3 %all-to-all-start = ((f32[8,296,128]{2,1,0:T(8,128)}), f32[8,296,128]{2,1,0:T(8,128)S(1)}, u32[]{:S(2)}, u32[]{:S(2)}) async-start(f32[8,296,128]{2,1,0:T(8,128)} %get-tuple-element.24), calls=%async_computation | async-start | bytes 2424832 | tf_op jit(solution)/shard_map/all_to_all | solution.py:316
  76.4 18.9 %all-to-all-start.2 = ((f32[8,256,128]{2,1,0:T(8,128)}), f32[8,256,128]{2,1,0:T(8,128)S(1)}, u32[]{:S(2)}, u32[]{:S(2)}) async-start(f32[8,256,128]{2,1,0:T(8,128)} %shard_map.71), calls=%async_computation.2 | async-start | bytes 2097152 | tf_op jit(solution)/shard_map/all_to_all | solution.py:316
  101.6 97.0 %all-to-all-start.3 = ((f32[32,64,128]{2,1,0:T(8,128)}), f32[32,64,128]{2,1,0:T(8,128)S(1)}, u32[]{:S(2)}, u32[]{:S(2)}) async-start(f32[32,64,128]{2,1,0:T(8,128)} %get-tuple-element.30), calls=%async_computation.3 | async-start | bytes 2097152 | tf_op jit(solution)/shard_map/all_to_all | solution.py:316
  106.7 32.3 %collective-permute-start = (f32[4,256,128]{2,1,0:T(8,128)S(1)}, f32[4,256,128]{2,1,0:T(8,128)S(1)}, u32[]{:S(2)}, u32[]{:S(2)}) collective-permute-start(f32[4,256,128]{2,1,0:T(8,128)S(1)} %get-tuple-element.52), channel_id=1, source_target_pairs={{0,1},{1,2},{2,3},{3,0},{4,5},{5,6},{6,7},{7,4},{8,9},{9,10},{10,1... | collective-permute-start | bytes 1572872 | tf_op jit(solution)/shard_map/ppermute | solution.py:322
  108.5 68.9 %collective-permute-start.1 = (f32[4,256,128]{2,1,0:T(8,128)S(1)}, f32[4,256,128]{2,1,0:T(8,128)S(1)}, u32[]{:S(2)}, u32[]{:S(2)}) collective-permute-start(f32[4,256,128]{2,1,0:T(8,128)S(1)} %get-tuple-element.51), channel_id=1, source_target_pairs={{0,2},{1,3},{2,0},{3,1},{4,6},{5,7},{6,4},{7,5},{8,10},{9,11},{10,... | collective-permute-start | bytes 1572872 | tf_op jit(solution)/shard_map/ppermute | solution.py:322
  110.9 66.5 %collective-permute-start.2 = (f32[4,256,128]{2,1,0:T(8,128)S(1)}, f32[4,256,128]{2,1,0:T(8,128)S(1)}, u32[]{:S(2)}, u32[]{:S(2)}) collective-permute-start(f32[4,256,128]{2,1,0:T(8,128)S(1)} %get-tuple-element.50), channel_id=1, source_target_pairs={{0,3},{1,0},{2,1},{3,2},{4,7},{5,4},{6,5},{7,6},{8,11},{9,8},{10,9... | collective-permute-start | bytes 1572872 | tf_op jit(solution)/shard_map/ppermute | solution.py:322
  113.1 65.1 %collective-permute-start.3 = (f32[8,4,16,128]{3,2,1,0:T(8,128)S(1)}, f32[8,4,16,128]{3,2,1,0:T(8,128)S(1)}, u32[]{:S(2)}, u32[]{:S(2)}) collective-permute-start(f32[8,4,16,128]{3,2,1,0:T(8,128)S(1)} %get-tuple-element.48), channel_id=1, source_target_pairs={{0,1},{1,2},{2,3},{3,0},{4,5},{5,6},{6,7},{7,4},{8,9},{9,10},{10,1... | collective-permute-start | bytes 786440 | tf_op jit(solution)/shard_map/ppermute | solution.py:378
  113.7 80.5 %collective-permute-start.4 = (f32[8,4,16,128]{3,2,1,0:T(8,128)S(1)}, f32[8,4,16,128]{3,2,1,0:T(8,128)S(1)}, u32[]{:S(2)}, u32[]{:S(2)}) collective-permute-start(f32[8,4,16,128]{3,2,1,0:T(8,128)S(1)} %get-tuple-element.47), channel_id=1, source_target_pairs={{0,2},{1,3},{2,0},{3,1},{4,6},{5,7},{6,4},{7,5},{8,10},{9,11},{10,... | collective-permute-start | bytes 786440 | tf_op jit(solution)/shard_map/ppermute | solution.py:378
  139.0 55.2 %collective-permute-start.5 = (f32[8,4,16,128]{3,2,1,0:T(8,128)S(1)}, f32[8,4,16,128]{3,2,1,0:T(8,128)S(1)}, u32[]{:S(2)}, u32[]{:S(2)}) collective-permute-start(f32[8,4,16,128]{3,2,1,0:T(8,128)S(1)} %get-tuple-element.46), channel_id=1, source_target_pairs={{0,3},{1,0},{2,1},{3,2},{4,7},{5,4},{6,5},{7,6},{8,11},{9,8},{10,9... | collective-permute-start | bytes 786440 | tf_op jit(solution)/shard_map/ppermute | solution.py:378
  253.3 27.6 %all-to-all-start.5 = ((f32[32,64,128]{2,1,0:T(8,128)}), f32[32,64,128]{2,1,0:T(8,128)S(1)}, u32[]{:S(2)}, u32[]{:S(2)}) async-start(f32[32,64,128]{2,1,0:T(8,128)} %get-tuple-element.37), calls=%async_computation.5 | async-start | bytes 2097152 | tf_op jit(solution)/shard_map/all_to_all | solution.py:316
  255.9 176.4 %all-gather.3.cloned.1.call-start = ((), (), s32[]{:S(2)}) async-start(), calls=%async_computation.8 | async-start | bytes 7077888 | tf_op jit(solution)/shard_map/all_gather | solution.py:496
  320.8 29.5 %all-to-all-start.7 = ((f32[32,64,128]{2,1,0:T(8,128)}), f32[32,64,128]{2,1,0:T(8,128)S(1)}, u32[]{:S(2)}, u32[]{:S(2)}) async-start(f32[32,64,128]{2,1,0:T(8,128)} %get-tuple-element.44), calls=%async_computation.7 | async-start | bytes 2097152 | tf_op jit(solution)/shard_map/all_to_all | solution.py:316
  356.2 16.6 %collective-permute-start.7 = (f32[2,2,256,128]{3,2,1,0:T(8,128)}, f32[2,2,256,128]{3,2,1,0:T(8,128)S(1)}, u32[]{:S(2)}, u32[]{:S(2)}) collective-permute-start(f32[2,2,256,128]{3,2,1,0:T(8,128)} %shard_map.77), channel_id=1, source_target_pairs={{0,1},{1,2},{2,3},{4,5},{5,6},{6,7},{8,9},{9,10},{10,11},{12,13},{... | collective-permute-start | bytes 1572872 | tf_op jit(solution)/shard_map/ppermute | solution.py:273
  361.3 17.0 %collective-permute-start.6 = (f32[2,2,256,128]{3,2,1,0:T(8,128)}, f32[2,2,256,128]{3,2,1,0:T(8,128)S(1)}, u32[]{:S(2)}, u32[]{:S(2)}) collective-permute-start(f32[2,2,256,128]{3,2,1,0:T(8,128)} %shard_map.77), channel_id=1, source_target_pairs={{1,0},{2,1},{3,2},{5,4},{6,5},{7,6},{9,8},{10,9},{11,10},{13,12},{... | collective-permute-start | bytes 1572872 | tf_op jit(solution)/shard_map/ppermute | solution.py:274
  367.0 17.2 %collective-permute-start.13 = (f32[2,2,256,128]{3,2,1,0:T(8,128)}, f32[2,2,256,128]{3,2,1,0:T(8,128)S(1)}, u32[]{:S(2)}, u32[]{:S(2)}) collective-permute-start(f32[2,2,256,128]{3,2,1,0:T(8,128)} %shard_map.78), channel_id=1, source_target_pairs={{0,1},{1,2},{2,3},{4,5},{5,6},{6,7},{8,9},{9,10},{10,11},{12,13},{... | collective-permute-start | bytes 1572872 | tf_op jit(solution)/shard_map/ppermute | solution.py:273
  371.6 16.9 %collective-permute-start.12 = (f32[2,2,256,128]{3,2,1,0:T(8,128)}, f32[2,2,256,128]{3,2,1,0:T(8,128)S(1)}, u32[]{:S(2)}, u32[]{:S(2)}) collective-permute-start(f32[2,2,256,128]{3,2,1,0:T(8,128)} %shard_map.78), channel_id=1, source_target_pairs={{1,0},{2,1},{3,2},{5,4},{6,5},{7,6},{9,8},{10,9},{11,10},{13,12},{... | collective-permute-start | bytes 1572872 | tf_op jit(solution)/shard_map/ppermute | solution.py:274
  372.9 22.4 %collective-permute-start.8 = (f32[2,2,256,128]{3,2,1,0:T(8,128)S(1)}, f32[2,2,256,128]{3,2,1,0:T(8,128)}, u32[]{:S(2)}, u32[]{:S(2)}) collective-permute-start(f32[2,2,256,128]{3,2,1,0:T(8,128)S(1)} %collective-permute-done.7), channel_id=1, source_target_pairs={{0,1},{1,2},{2,3},{4,5},{5,6},{6,7},{8,9},{9,10},{10,11},{12,13},{... | collective-permute-start | bytes 1572872 | tf_op jit(solution)/shard_map/ppermute | solution.py:273
  378.2 25.7 %collective-permute-start.10 = (f32[2,2,256,128]{3,2,1,0:T(8,128)S(1)}, f32[2,2,256,128]{3,2,1,0:T(8,128)}, u32[]{:S(2)}, u32[]{:S(2)}) collective-permute-start(f32[2,2,256,128]{3,2,1,0:T(8,128)S(1)} %collective-permute-done.6), channel_id=1, source_target_pairs={{1,0},{2,1},{3,2},{5,4},{6,5},{7,6},{9,8},{10,9},{11,10},{13,12},{... | collective-permute-start | bytes 1572872 | tf_op jit(solution)/shard_map/ppermute | solution.py:274
  384.1 22.4 %collective-permute-start.14 = (f32[2,2,256,128]{3,2,1,0:T(8,128)S(1)}, f32[2,2,256,128]{3,2,1,0:T(8,128)S(1)}, u32[]{:S(2)}, u32[]{:S(2)}) collective-permute-start(f32[2,2,256,128]{3,2,1,0:T(8,128)S(1)} %collective-permute-done.13), channel_id=1, source_target_pairs={{0,1},{1,2},{2,3},{4,5},{5,6},{6,7},{8,9},{9,10},{10,11},{12,13},{... | collective-permute-start | bytes 1572872 | tf_op jit(solution)/shard_map/ppermute | solution.py:273
  388.5 22.6 %collective-permute-start.16 = (f32[2,2,256,128]{3,2,1,0:T(8,128)S(1)}, f32[2,2,256,128]{3,2,1,0:T(8,128)}, u32[]{:S(2)}, u32[]{:S(2)}) collective-permute-start(f32[2,2,256,128]{3,2,1,0:T(8,128)S(1)} %collective-permute-done.12), channel_id=1, source_target_pairs={{1,0},{2,1},{3,2},{5,4},{6,5},{7,6},{9,8},{10,9},{11,10},{13,12},{... | collective-permute-start | bytes 1572872 | tf_op jit(solution)/shard_map/ppermute | solution.py:274
  395.3 22.6 %collective-permute-start.9 = (f32[2,2,256,128]{3,2,1,0:T(8,128)}, f32[2,2,256,128]{3,2,1,0:T(8,128)}, u32[]{:S(2)}, u32[]{:S(2)}) collective-permute-start(f32[2,2,256,128]{3,2,1,0:T(8,128)} %collective-permute-done.8), channel_id=1, source_target_pairs={{0,1},{1,2},{2,3},{4,5},{5,6},{6,7},{8,9},{9,10},{10,11},{12,13},{... | collective-permute-start | bytes 1572872 | tf_op jit(solution)/shard_map/ppermute | solution.py:273
  403.9 18.3 %collective-permute-start.11 = (f32[2,2,256,128]{3,2,1,0:T(8,128)}, f32[2,2,256,128]{3,2,1,0:T(8,128)S(1)}, u32[]{:S(2)}, u32[]{:S(2)}) collective-permute-start(f32[2,2,256,128]{3,2,1,0:T(8,128)} %collective-permute-done.10), channel_id=1, source_target_pairs={{1,0},{2,1},{3,2},{5,4},{6,5},{7,6},{9,8},{10,9},{11,10},{13,12},{... | collective-permute-start | bytes 1572872 | tf_op jit(solution)/shard_map/ppermute | solution.py:274
  406.5 20.8 %collective-permute-start.15 = (f32[2,2,256,128]{3,2,1,0:T(8,128)S(1)}, f32[2,2,256,128]{3,2,1,0:T(8,128)S(1)}, u32[]{:S(2)}, u32[]{:S(2)}) collective-permute-start(f32[2,2,256,128]{3,2,1,0:T(8,128)S(1)} %collective-permute-done.14), channel_id=1, source_target_pairs={{0,1},{1,2},{2,3},{4,5},{5,6},{6,7},{8,9},{9,10},{10,11},{12,13},{... | collective-permute-start | bytes 1572872 | tf_op jit(solution)/shard_map/ppermute | solution.py:273
  411.0 20.4 %collective-permute-start.17 = (f32[2,2,256,128]{3,2,1,0:T(8,128)}, f32[2,2,256,128]{3,2,1,0:T(8,128)S(1)}, u32[]{:S(2)}, u32[]{:S(2)}) collective-permute-start(f32[2,2,256,128]{3,2,1,0:T(8,128)} %collective-permute-done.16), channel_id=1, source_target_pairs={{1,0},{2,1},{3,2},{5,4},{6,5},{7,6},{9,8},{10,9},{11,10},{13,12},{... | collective-permute-start | bytes 1572872 | tf_op jit(solution)/shard_map/ppermute | solution.py:274
  (16 other events, 217.0 us)
Sparse Core Ops, SparseCore 0:
  320.9 52.1 all-gather.2

commit v2 on v1

--- a/solution.py
+++ b/solution.py
@@ -9,6 +9,7 @@
 
 
 EPSILON = 1e-06
+LIMIT = 24 * 2**20
 SUBLANES = 8
 f32 = jnp.float32
 bf16 = jnp.bfloat16
@@ -47,15 +48,19 @@
     return pl.BlockSpec(shape, lambda *_: (0,) * len(shape))
 
 
+def whole(space):
+    return pl.BlockSpec(memory_space=space)
+
+
 def squares(x):
     return jnp.sum(x * x, axis=0, keepdims=True)
 
 
-def first_kernel(bl, y, foot, *refs, parts, own, step):
+def first_kernel(bl, y, foot, *refs, parts, own, step, extra):
     t0s, t1s = refs[:step], refs[step:2 * step]
-    pos, base_out, pay = refs[2 * step:]
+    base_out, pay = refs[2 * step:]
     at = pl.program_id(0) * step
-    count = pl.num_programs(0) * step
+    count = bl.shape[0]
     kb = foot.shape[3]
     for i in range(step):
         f0, f1 = split(foot[i, 0]), split(foot[i, 1])
@@ -71,8 +76,13 @@
 
     @pl.when(at == 0)
     def _():
-        start = pay.shape[1] - pos.shape[0]
-        pay[:, start:, :] = jnp.broadcast_to(pos[...][None], (parts,) + pos.shape)
+        shape = (extra, kb)
+        where = lax.broadcasted_iota(jnp.int32, shape, 0) * kb + lax.broadcasted_iota(jnp.int32, shape, 1)
+        listing = jnp.zeros(shape, jnp.int32)
+        for p in range(count):
+            for g in range(2):
+                listing = jnp.where(where == 2 * p + g, bl[p, g], listing)
+        pay[:, pay.shape[1] - extra:, :] = jnp.broadcast_to(listing.astype(f32)[None], (parts,) + shape)
 
 
 def second_kernel(base, foot, rx, pay, *, parts, own, step):
@@ -150,14 +160,11 @@
         scratch.append(pltpu.VMEM(norms_shape, f32))
     return pl.pallas_call(
         functools.partial(owner_kernel, group=group, per=per, own=own, outs=outs, outper=outper, other=other),
-        grid_spec=pltpu.PrefetchScalarGridSpec(
-            num_scalar_prefetch=3,
-            grid=(1,),
-            in_specs=[full_spec(x.shape) for x in (rx, before, *extra)],
-            out_specs=[full_spec(shape) for shape in shapes],
-            scratch_shapes=scratch,
-        ),
+        in_specs=[whole(pltpu.SMEM)] * 3 + [whole(pltpu.VMEM)] * (2 + len(extra)),
+        out_specs=[whole(pltpu.VMEM)] * len(shapes),
+        scratch_shapes=scratch,
         out_shape=[jax.ShapeDtypeStruct(shape, f32) for shape in shapes],
+        compiler_params=pltpu.CompilerParams(vmem_limit_bytes=LIMIT),
         name="owner",
     )(*tables, rx, before, *extra)
 
@@ -176,7 +183,7 @@
     for s in range(ntm):
         piece = terms[s * npix * own:(s + 1) * npix * own].reshape(npix, own, kb)
         to = lax.rem(me + (ntm - s), ntm)
-        pay[:, to, pl.ds(pl.multiple_of(p * own, SUBLANES), own), :] = piece
+        pay[:, to, p * own:(p + 1) * own, :] = piece
 
 
 def footprint_phase(residual, f0, f1, t0, t1):
@@ -190,70 +197,52 @@
     return residual, n0, n1, s1
 
 
-def merge_kernel(me_ref, *refs, ntm, step):
+def third_kernel(*refs, ntm):
     ys, t0s = refs[:ntm], refs[ntm:2 * ntm]
-    foot, residual_out, t0_out = refs[2 * ntm:]
-    kb = foot.shape[3]
-    for i in range(step):
+    rx1, foot, residual_out, foot_out, t0_out, t1_out, pay = refs[2 * ntm:]
+    me = lax.axis_index("tm")
+    count, kb = foot.shape[0], foot.shape[3]
+    own = (pay.shape[2] - up8(2 * count)) // count
+    for i in range(count):
+        f0, f1 = foot[i, 0], foot[i, 1]
         y = jnp.concatenate([ref[i] for ref in ys], axis=1)
         t0 = jnp.concatenate([ref[:, i].reshape(ref.shape[0] * ref.shape[2], kb) for ref in t0s], axis=0)
-        residual_out[i] = y - rows_by_rows(split(foot[i, 0]), split(t0))
-        t0_out[i] = t0
-
-
-def third_kernel(me_ref, part, t0_in, rx1, foot, residual_out, foot_out, t1_out, pay, *, ntm, step):
-    me = me_ref[0]
-    at = pl.program_id(0) * step
-    count = pl.num_programs(0) * step
-    for i in range(step):
-        f0, f1 = foot[i, 0], foot[i, 1]
         t1 = incoming(rx1, i, me, ntm)
-        residual = part[i] - rows_by_rows(split(f1), split(t1))
-        residual, n0, n1, s1 = footprint_phase(residual, f0, f1, t0_in[i], t1)
+        residual = y - rows_by_rows(split(f0), split(t0)) - rows_by_rows(split(f1), split(t1))
+        residual, n0, n1, s1 = footprint_phase(residual, f0, f1, t0, t1)
         residual = residual - rows_by_rows(split(n1 - f1), s1)
         residual_out[i] = residual
         foot_out[i, 0] = n0
         foot_out[i, 1] = n1
+        t0_out[i] = t0
         t1_out[i] = t1
-        outgoing(pay, rows_by_columns(split(residual), split(n0), 0), at + i, me, ntm)
-        own = (pay.shape[2] - up8(2 * count)) // count
+        outgoing(pay, rows_by_columns(split(residual), split(n0), 0), i, me, ntm)
         for g, new in enumerate((n0, n1)):
-            norm = jnp.broadcast_to(squares(new)[None, None], pay.shape[:2] + (1, new.shape[1]))
-            pay[:, :, pl.ds(count * own + g * count + at + i, 1), :] = norm
-
-
-def ahead_kernel(residual, foot, terms_out, gram_out, *, step):
-    for i in range(step):
-        f1 = split(foot[i, 1])
-        terms_out[i] = rows_by_columns(split(residual[i]), f1, 0)
-        gram_out[i] = rows_by_columns(split(foot[i, 0]), f1, 0)
-
-
-def fourth_kernel(me_ref, terms, gram, told, rx, change_out, pay, *, ntm, step):
-    me = me_ref[0]
-    at = pl.program_id(0) * step
-    for i in range(step):
+            norm = jnp.broadcast_to(squares(new)[None, None], pay.shape[:2] + (1, kb))
+            row = count * own + g * count + i
+            pay[:, :, row:row + 1, :] = norm
+
+
+def fourth_kernel(residual_in, foot, told, rx, residual_out, pay, *, ntm):
+    me = lax.axis_index("tm")
+    for i in range(told.shape[0]):
         change = incoming(rx, i, me, ntm) - told[i]
-        change_out[i] = change
-        new = terms[i] - rows_by_columns(split(change), split(gram[i]))
-        outgoing(pay, new, at + i, me, ntm)
-
-
-def late_kernel(residual, foot, change, residual_out, *, step):
-    for i in range(step):
-        residual_out[i] = residual[i] - rows_by_rows(split(foot[i, 0]), split(change[i]))
-
-
-def last_kernel(me_ref, residual_in, foot, told, rx0, rx1, foot_out, *, ntm, step):
-    me = me_ref[0]
-    for i in range(step):
+        residual = residual_in[i] - rows_by_rows(split(foot[i, 0]), split(change))
+        residual_out[i] = residual
+        outgoing(pay, rows_by_columns(split(residual), split(foot[i, 1]), 0), i, me, ntm)
+
+
+def last_kernel(residual_in, foot, told, rx0, rx1, foot_out, *, ntm, skip):
+    me = lax.axis_index("tm")
+    for o in range(foot_out.shape[0]):
+        i = skip + o
         f0, f1 = foot[i, 0], foot[i, 1]
         t0 = incoming(rx0, i, me, ntm)
         t1 = incoming(rx1, i, me, ntm)
         residual = residual_in[i] - rows_by_rows(split(f1), split(t1 - told[i]))
         _, n0, n1, _ = footprint_phase(residual, f0, f1, t0, t1)
-        foot_out[i, 0] = n0
-        foot_out[i, 1] = n1
+        foot_out[o, 0] = n0
+        foot_out[o, 1] = n1
 
 
 def flip_kernel(rx, out):
@@ -262,8 +251,61 @@
         out[j] = rx[:, j].reshape(npix * own, kb).T
 
 
+def early_kernel(*refs, n, count, axis):
+    chunks, rest, out, sems = refs[:count], refs[count:-2], refs[-2], refs[-1]
+    me = lax.axis_index(axis)
+    per = chunks[0].shape[0]
+    from_left, from_right = rest[:(n - 2) * count], rest[(n - 2) * count:]
+
+    def copy(source, s, c):
+        place = lax.rem(me + s, n) * (count * per) + c * per
+        return pltpu.make_async_copy(source, out.at[pl.ds(place, per)], sems.at[s, c])
+
+    def every(act):
+        for c in range(count):
+            act(copy(chunks[c], 0, c))
+            for s in range(1, n):
+                if s <= n - 2:
+
+                    @pl.when(me + s < n)
+                    def _():
+                        act(copy(from_right[(s - 1) * count + c], s, c))
+
+                if s >= 2:
+
+                    @pl.when(me + s >= n)
+                    def _():
+                        act(copy(from_left[(n - s - 1) * count + c], s, c))
+
+    every(lambda one: one.start())
+    every(lambda one: one.wait())
+
+
+def ends_kernel(before, *refs, n, count, axis):
+    from_left, from_right, out, sems = refs[:count], refs[count:2 * count], refs[-2], refs[-1]
+    me = lax.axis_index(axis)
+    per = from_left[0].shape[0]
+
+    def move(sources, place):
+        for c in range(count):
+            pltpu.make_async_copy(
+                sources[c], out.at[pl.ds((place * count + c) * per, per)], sems.at[c]
+            ).start()
+        for c in range(count):
+            pltpu.make_async_copy(
+                sources[c], out.at[pl.ds((place * count + c) * per, per)], sems.at[c]
+            ).wait()
+
+    @pl.when(me == 0)
+    def _():
+        move(from_right, n - 1)
+
+    @pl.when(me == n - 1)
+    def _():
+        move(from_left, 0)
+
+
 def line_gather(chunks, axis, n):
-    me = lax.axis_index(axis)
     size = sum(x.shape[0] for x in chunks)
     rest = chunks[0].shape[1:]
     left, right = list(chunks), list(chunks)
@@ -273,15 +315,29 @@
             left[c] = lax.ppermute(left[c], axis, [(j, j + 1) for j in range(n - 1)])
             right[c] = lax.ppermute(right[c], axis, [(j, j - 1) for j in range(1, n)])
             from_left[s, c], from_right[s, c] = left[c], right[c]
-    out = jnp.zeros((n * size,) + rest, chunks[0].dtype)
-    offset = 0
-    for c, x in enumerate(chunks):
-        out = lax.dynamic_update_slice_in_dim(out, x, me * size + offset, 0)
-        for s in range(1, n):
-            piece = jnp.where(me + s < n, from_right[s, c], from_left[n - s, c])
-            out = lax.dynamic_update_slice_in_dim(out, piece, lax.rem(me + s, n) * size + offset, 0)
-        offset += x.shape[0]
-    return out
+    shape = jax.ShapeDtypeStruct((n * size,) + rest, f32)
+    early = [s for s in range(1, n - 1)]
+    sources = list(chunks) + [d[s, c] for d in (from_left, from_right) for s in early for c in range(len(chunks))]
+    out = pl.pallas_call(
+        functools.partial(early_kernel, n=n, count=len(chunks), axis=axis),
+        in_specs=[whole(pltpu.VMEM)] * len(sources),
+        out_specs=whole(pltpu.HBM),
+        out_shape=shape,
+        scratch_shapes=[pltpu.SemaphoreType.DMA((n, len(chunks)))],
+        compiler_params=pltpu.CompilerParams(vmem_limit_bytes=LIMIT),
+        name="early",
+    )(*sources)
+    ends = [d[n - 1, c] for d in (from_left, from_right) for c in range(len(chunks))]
+    return pl.pallas_call(
+        functools.partial(ends_kernel, n=n, count=len(chunks), axis=axis),
+        in_specs=[whole(pltpu.HBM)] + [whole(pltpu.VMEM)] * len(ends),
+        out_specs=whole(pltpu.HBM),
+        out_shape=shape,
+        input_output_aliases={0: 0},
+        scratch_shapes=[pltpu.SemaphoreType.DMA((len(chunks),))],
+        compiler_params=pltpu.CompilerParams(vmem_limit_bytes=LIMIT),
+        name="ends",
+    )(out, *ends)
 
 
 def local(recording, footprints, traces, block_list, block_order, *, npix, ntm):
@@ -296,7 +352,7 @@
     pix, tm = lax.axis_index("pix"), lax.axis_index("tm")
     me = jnp.reshape(tm, (1,)).astype(jnp.int32)
 
-    def kernel(body, grid, in_specs, out_specs, out_shape, prefetch=0, scratch=(), **static):
+    def kernel(body, grid, in_specs, out_specs, out_shape, prefetch=0, scratch=(), limit=None, **static):
         return pl.pallas_call(
             functools.partial(body, **static),
             grid_spec=pltpu.PrefetchScalarGridSpec(
@@ -307,7 +363,20 @@
                 scratch_shapes=scratch,
             ),
             out_shape=out_shape,
+            compiler_params=pltpu.CompilerParams(vmem_limit_bytes=limit),
         )
+
+    def resident(body, out_shape, **static):
+        def run(*operands):
+            return pl.pallas_call(
+                functools.partial(body, **static),
+                in_specs=[whole(pltpu.VMEM)] * len(operands),
+                out_specs=jax.tree.map(lambda _: whole(pltpu.VMEM), out_shape),
+                out_shape=out_shape,
+                compiler_params=pltpu.CompilerParams(vmem_limit_bytes=LIMIT),
+            )(*operands)
+
+        return run
 
     def array(*shape):
         return jax.ShapeDtypeStruct(shape, f32)
@@ -322,9 +391,6 @@
         y_pieces.append(lax.ppermute(piece, "tm", [(j, (j + s) % ntm) for j in range(ntm)]) if s else piece)
 
     pos_rows = up8(-(-count * groups // kb))
-    pos_row = jnp.pad(
-        block_list.astype(f32).reshape(-1), (0, pos_rows * kb - count * groups)
-    ).reshape(pos_rows, kb)
     place = jnp.zeros((blocks,), jnp.int32).at[block_order].set(jnp.arange(blocks, dtype=jnp.int32))
 
     step = divisor(count, (4, 2, 1))
@@ -337,12 +403,11 @@
 
     base, pay = kernel(
         first_kernel, (count // step,),
-        [patch_spec, foot_spec] + [block_spec(i, g) for g in range(groups) for i in range(step)]
-        + [full_spec(pos_row.shape)],
+        [patch_spec, foot_spec] + [block_spec(i, g) for g in range(groups) for i in range(step)],
         [patch_spec, full_spec((npix, rows + pos_rows, kb))],
         [array(count, voxels, frames), array(npix, rows + pos_rows, kb)],
-        prefetch=1, parts=npix, own=own, step=step,
-    )(block_list, recording, footprints, *[traces] * (groups * step), pos_row)
+        prefetch=1, parts=npix, own=own, step=step, extra=pos_rows,
+    )(block_list, recording, footprints, *[traces] * (groups * step))
     got = exchange(pay, "pix")
 
     several = divisor(bpg, (8, 4, 2, 1))
@@ -363,6 +428,7 @@
         )(block_order, whereabouts, *[traces] * several)
 
     before0, before1 = prepared(0), prepared(1)
+    own_foot = lax.dynamic_slice_in_dim(footprints, tm * share, share, 0)
 
     listing = got[:, rows:, :].reshape(npix, -1)[:, :count * groups].reshape(npix * count, groups)
     tables = (listing.astype(jnp.int32), place, block_order)
@@ -397,65 +463,20 @@
 
     rx1 = landed(spread(back))
 
-    step = divisor(share, (2, 1))
-    grid = (share // step,)
-    share_spec = pl.BlockSpec((step, voxels, frames), lambda p, *_: (p, 0, 0))
-    part_spec = pl.BlockSpec((npix, step, own, kb), lambda p, *_: (0, p, 0, 0))
-    rx_spec = pl.BlockSpec((npix, ntm, step, own, kb), lambda p, *_: (0, 0, p, 0, 0))
-    residual_spec = pl.BlockSpec((step, voxels, every), lambda p, *_: (p, 0, 0))
-    trace_spec = pl.BlockSpec((step, every, kb), lambda p, *_: (p, 0, 0))
-    gram_spec = pl.BlockSpec((step, kb, kb), lambda p, *_: (p, 0, 0))
-    foot_spec = pl.BlockSpec((step, groups, voxels, kb), lambda p, *_: (p, 0, 0, 0))
-    own_foot_spec = pl.BlockSpec(
-        (step, groups, voxels, kb), lambda p, me: (me[0] * (share // step) + p, 0, 0, 0)
-    )
     residual_type, trace_type = array(share, voxels, every), array(share, every, kb)
-    foot_type = array(share, groups, voxels, kb)
     wide = (npix, ntm, share * own + up8(groups * share), kb)
     narrow = (npix, ntm, share * own, kb)
-
-    part, t0_old = kernel(
-        merge_kernel, grid,
-        [share_spec] * ntm + [part_spec] * ntm + [own_foot_spec],
-        [residual_spec, trace_spec],
-        [residual_type, trace_type],
-        prefetch=1, ntm=ntm, step=step,
-    )(me, *y_pieces, *t0_pieces, footprints)
-    residual, foot, t1_old, pay = kernel(
-        third_kernel, grid,
-        [residual_spec, trace_spec, rx_spec, own_foot_spec],
-        [residual_spec, foot_spec, trace_spec, full_spec(wide)],
-        [residual_type, foot_type, trace_type, array(*wide)],
-        prefetch=1, ntm=ntm, step=step,
-    )(me, part, t0_old, rx1, footprints)
+    residual, foot, t0_old, t1_old, pay = resident(
+        third_kernel, [residual_type, array(share, groups, voxels, kb), trace_type, trace_type, array(*wide)], ntm=ntm
+    )(*y_pieces, *t0_pieces, rx1, own_foot)
 
     got = spread(pay)
-    terms, gram = kernel(
-        ahead_kernel, grid,
-        [residual_spec, foot_spec],
-        [trace_spec, gram_spec],
-        [trace_type, array(share, kb, kb)],
-        step=step,
-    )(residual, foot)
     after0, back, norms1 = owner(
         tables, got, after0, (), group=0, per=share, outs=everyone, outper=share, other="norms"
     )
     rx0 = landed(spread(back))
-    change, pay = kernel(
-        fourth_kernel, grid,
-        [trace_spec, gram_spec, trace_spec, rx_spec],
-        [trace_spec, full_spec(narrow)],
-        [trace_type, array(*narrow)],
-        prefetch=1, ntm=ntm, step=step,
-    )(me, terms, gram, t0_old, rx0)
+    residual, pay = resident(fourth_kernel, [residual_type, array(*narrow)], ntm=ntm)(residual, foot, t0_old, rx0)
     got = spread(pay)
-    residual = kernel(
-        late_kernel, grid,
-        [residual_spec, foot_spec, trace_spec],
-        residual_spec,
-        residual_type,
-        step=step,
-    )(residual, foot, change)
     after1, back, final = owner(
         tables, got, after1, (norms1, after0), group=1, per=share, outs=everyone, outper=share, other="final"
     )
@@ -463,34 +484,10 @@
 
     halves = divisor(share, (2, 1))
     half = share // halves
-    chunks = []
-    for c in range(halves):
-        step = divisor(half, (2, 1))
-        skip = c * half // step
-
-        def at(spec, axis):
-            shape, index = spec
-
-            def moved(p, me, index=index, skip=skip, axis=axis):
-                return tuple(skip + p if a == axis else 0 for a in range(index))
-
-            return pl.BlockSpec(shape, moved)
-
-        chunks.append(
-            kernel(
-                last_kernel, (half // step,),
-                [
-                    at(((step, voxels, every), 3), 0),
-                    at(((step, groups, voxels, kb), 4), 0),
-                    at(((step, every, kb), 3), 0),
-                    at(((npix, ntm, step, own, kb), 5), 2),
-                    at(((npix, ntm, step, own, kb), 5), 2),
-                ],
-                pl.BlockSpec((step, groups, voxels, kb), lambda p, *_: (p, 0, 0, 0)),
-                array(half, groups, voxels, kb),
-                prefetch=1, ntm=ntm, step=step,
-            )(me, residual, foot, t1_old, rx0, rx1)
-        )
+    chunks = [
+        resident(last_kernel, array(half, groups, voxels, kb), ntm=ntm, skip=c * half)(residual, foot, t1_old, rx0, rx1)
+        for c in range(halves)
+    ]
     footprints_out = line_gather(chunks, "tm", ntm)
 
     gathered = lax.all_gather(final, "pix", axis=0)
@@ -499,6 +496,7 @@
         [pl.BlockSpec((npix, several, own, kb), lambda j: (0, j, 0, 0))],
         pl.BlockSpec((several, kb, frames), lambda j: (j, 0, 0)),
         array(blocks, kb, frames),
+        limit=LIMIT,
     )(gathered)
     return footprints_out, traces_out
 

time: 452 us -> 431 us (0.954)
  blocking collectives: 88.1 us -> 143 us
  waiting for transfers between devices: 164 us -> 133 us
  Pallas kernels: 94.8 us -> 64.8 us
  starting transfers between devices: 63.9 us -> 54.7 us
  other arithmetic: 8.94 us -> 2.44 us
    all_to_all x3 -> x5, blocking collectives: 88.1 us -> 143 us  [exchange(): return lax.all_to_all(x, axes, 0, 0, tiled=True)]
    all_to_all x5 -> x3, waiting for transfers between devices: 62 us -> 19.8 us  [exchange(): return lax.all_to_all(x, axes, 0, 0, tiled=True)]
    pallas_call x7 -> x6, Pallas kernels: 32.4 us -> 15.5 us  [the longest x4 12.8 us: run(): pl.pallas_call(functools.partial(body, **static), in_specs=[whole(pltpu.V...]
    pallas_call x4, Pallas kernels: 22.4 us -> 13 us  [owner(): pl.pallas_call(functools.partial(owner_kernel, group=group, per=per, own=...]
    ppermute x6, waiting for transfers between devices: 20.4 us -> 28 us  [line_gather(): left[c] = lax.ppermute(left[c], axis, [(j, j + 1) for j in range(n - 1)])]
    all_to_all x5 -> x3, starting transfers between devices: 20.1 us -> 12.5 us  [exchange(): return lax.all_to_all(x, axes, 0, 0, tiled=True)]
    dynamic_update_slice x6 -> x0, other arithmetic: 7.22 us -> none  [line_gather(): lax.dynamic_update_slice_in_dim(out, piece, lax.rem(me + s, n) * size + o...]
    unnamed x35 -> x45, local copies, waits for them, and re-layouts: 7.08 us -> 14.1 us
  transfers between devices with their start and end apart: 24 -> 22, of which waited for: 15 -> 13; matrix products, arithmetic and copies ran while one was open for 3% -> 1% of each run, Pallas kernels for 7% -> 4%
where the time goes in v2:
time: 431 us; the launch traced here: 429 us
  blocking collectives  143 us (33%)
  waiting for transfers between devices  133 us (31%)
  Pallas kernels  64.8 us (15%)
  starting transfers between devices  54.7 us (13%)
  local copies, waits for them, and re-layouts  17.2 us (4%)
  between operations  14.4 us (3%)
    all_to_all x5, blocking collectives, exchange(): return lax.all_to_all(x, axes, 0, 0, tiled=True)  143 us
    ppermute x6, waiting for transfers between devices, local(): lax.ppermute(piece, 'tm', [(j, (j + s) % ntm) for j in range(ntm)])  76 us
    ppermute x6, waiting for transfers between devices, line_gather(): left[c] = lax.ppermute(left[c], axis, [(j, j + 1) for j in range(n - 1)])  28 us
    ppermute x6, starting transfers between devices, line_gather(): left[c] = lax.ppermute(left[c], axis, [(j, j + 1) for j in range(n - 1)])  27.2 us
    all_to_all x3, waiting for transfers between devices, exchange(): return lax.all_to_all(x, axes, 0, 0, tiled=True)  19.8 us
    unnamed x45, local copies, waits for them, and re-layouts  14.1 us
    pallas_call x4, Pallas kernels, owner(): pl.pallas_call(functools.partial(owner_kernel, group=group, per=per, own=...  13 us
    pallas_call x4, Pallas kernels, run(): pl.pallas_call(functools.partial(body, **static), in_specs=[whole(pltpu.V...  12.8 us
  transfers between devices with their start and end apart: 22, of which 13 were waited for; matrix products, arithmetic and copies ran while one was open for 1% of the time, Pallas kernels for 4%

profile of v2, /device:TPU:0, one launch (start us, length us, event | category | flops | bytes accessed | tf_op | source)
XLA Modules:
  0.0 429.0 jit_solution(9067676020045891337)
XLA Ops:
  8.5 10.2 %shard_map.68 = (f32[16,256,128]{2,1,0:T(8,128)}, f32[8,296,128]{2,1,0:T(8,128)}) custom-call(s32[16,2]{1,0:T(8,128)} %copy.10.bl, bf16[16,256,128]{2,1,0:T(8,128)(2,1)} %y.1, f32[16,2,256,128]{3,2,1,0:T(8,128)} %foot.3, f32[96,128,128]{2,1,0:T(8,128)} %refs_7_.5, f32[96,128,128]{2,1,0:T(8,128)} %refs_7_.5, f32[96,128,128]{2,1,0:T(8,128)} %refs_7_.5, ...), custom_call_target="tpu_custom_call" | custom-call | tf_op jit(solution)/shard_map/pallas_call | solution.py:404
  18.7 4.9 %all-to-all-start = ((f32[8,296,128]{2,1,0:T(8,128)}), f32[8,296,128]{2,1,0:T(8,128)S(1)}, u32[]{:S(2)}, u32[]{:S(2)}) async-start(f32[8,296,128]{2,1,0:T(8,128)} %get-tuple-element.21), calls=%async_computation | async-start | bytes 2424832 | tf_op jit(solution)/shard_map/all_to_all | solution.py:385
  23.6 5.8 %shard_map.69.before = f32[48,16,128]{2,1,0:T(8,128)} custom-call(s32[96]{0:T(128)} %order.11, s32[1]{0:T(128)} %bitcast.pix, f32[96,128,128]{2,1,0:T(8,128)} %refs_7_.5, f32[96,128,128]{2,1,0:T(8,128)} %refs_7_.5, f32[96,128,128]{2,1,0:T(8,128)} %refs_7_.5, f32[96,128,128]{2,1,0:T(8,128)} %refs_7_.5, f32[96,128,128]{2,1,0:T(8,128)} %refs_7_.5, ...), custom_call_target="tpu_custom_call" | custom-call | tf_op jit(solution)/shard_map/pallas_call | solution.py:422
  30.3 10.4 %all-to-all-done.rx = f32[8,296,128]{2,1,0:T(8,128)S(1)} async-done(((f32[8,296,128]{2,1,0:T(8,128)}), f32[8,296,128]{2,1,0:T(8,128)S(1)}, u32[]{:S(2)}, u32[]{:S(2)}) %all-to-all-start) | async-done | bytes 1212448 | tf_op jit(solution)/shard_map/all_to_all | solution.py:385
  44.5 18.5 %all_to_all.40 = f32[8,256,128]{2,1,0:T(8,128)} all-to-all(f32[8,256,128]{2,1,0:T(8,128)S(1)} %get-tuple-element.22), channel_id=1, replica_groups=mesh['pix'=8,'tm'=4] {'pix'}, dimensions={0} | all-to-all | bytes 2097152 | tf_op jit(solution)/shard_map/all_to_all | solution.py:385
  63.0 7.9 %shard_map.70 = f32[8,256,128]{2,1,0:T(8,128)} custom-call(f32[16,256,128]{2,1,0:T(8,128)} %get-tuple-element.23.base, f32[16,2,256,128]{3,2,1,0:T(8,128)} %foot.3, f32[8,16,16,128]{3,2,1,0:T(8,128)} %bitcast.22), custom_call_target="tpu_custom_call" | custom-call | tf_op jit(solution)/shard_map/pallas_call | solution.py:446
  74.5 5.8 %shard_map.71.before = f32[48,16,128]{2,1,0:T(8,128)} custom-call(s32[96]{0:T(128)} %order.11, s32[1]{0:T(128)} %bitcast.pix, f32[96,128,128]{2,1,0:T(8,128)} %refs_7_.5, f32[96,128,128]{2,1,0:T(8,128)} %refs_7_.5, f32[96,128,128]{2,1,0:T(8,128)} %refs_7_.5, f32[96,128,128]{2,1,0:T(8,128)} %refs_7_.5, f32[96,128,128]{2,1,0:T(8,128)} %refs_7_.5, ...), custom_call_target="tpu_custom_call" | custom-call | tf_op jit(solution)/shard_map/pallas_call | solution.py:422
  80.3 9.5 %all-to-all-done.2.rx = f32[8,256,128]{2,1,0:T(8,128)S(1)} async-done(((f32[8,256,128]{2,1,0:T(8,128)}), f32[8,256,128]{2,1,0:T(8,128)S(1)}, u32[]{:S(2)}, u32[]{:S(2)}) %all-to-all-start.2) | async-done | bytes 1048608 | tf_op jit(solution)/shard_map/all_to_all | solution.py:385
  109.4 23.2 %collective-permute-done.refs_1_ = f32[4,256,128]{2,1,0:T(8,128)S(1)} collective-permute-done((f32[4,256,128]{2,1,0:T(8,128)S(1)}, f32[4,256,128]{2,1,0:T(8,128)S(1)}, u32[]{:S(2)}, u32[]{:S(2)}) %collective-permute-start) | collective-permute-done | bytes 524320 | tf_op jit(solution)/shard_map/ppermute | solution.py:391
  134.3 36.7 %collective-permute-done.1.refs_2_ = f32[4,256,128]{2,1,0:T(8,128)S(1)} collective-permute-done((f32[4,256,128]{2,1,0:T(8,128)}, f32[4,256,128]{2,1,0:T(8,128)S(1)}, u32[]{:S(2)}, u32[]{:S(2)}) %collective-permute-start.1) | collective-permute-done | bytes 524320 | tf_op jit(solution)/shard_map/ppermute | solution.py:391
  171.8 16.1 %collective-permute-done.4.refs_6_ = f32[8,4,16,128]{3,2,1,0:T(8,128)} collective-permute-done((f32[8,4,16,128]{3,2,1,0:T(8,128)}, f32[8,4,16,128]{3,2,1,0:T(8,128)}, u32[]{:S(2)}, u32[]{:S(2)}) %collective-permute-start.4) | collective-permute-done | bytes 262176 | tf_op jit(solution)/shard_map/ppermute | solution.py:444
  191.1 7.3 %shard_map.72 = (f32[4,256,512]{2,1,0:T(8,128)S(1)}, f32[4,2,256,128]{3,2,1,0:T(8,128)S(1)}, f32[4,512,128]{2,1,0:T(8,128)S(1)}, f32[4,512,128]{2,1,0:T(8,128)S(1)}, f32[8,4,72,128]{3,2,1,0:T(8,128)S(1)}) custom-call(f32[4,256,128]{2,1,0:T(8,128)S(1)} %copy-done.5, f32[4,256,128]{2,1,0:T(8,128)S(1)} %copy-done.11, f32[4,256,128]{2,1,0:T(8,128)S(1)} %copy-done.13, ...), custom_call_target="tpu_custom_call" | custom-call | tf_op jit(solution)/shard_map/pallas_call | solution.py:371
  198.4 38.7 %all_to_all.41.rx = f32[32,72,128]{2,1,0:T(8,128)S(1)} all-to-all(f32[32,72,128]{2,1,0:T(8,128)S(1)} %bitcast.20), channel_id=1, replica_groups=mesh['pix'=8,'tm'=4] {'pix','tm'}, dimensions={0} | all-to-all | bytes 2359296 | tf_op jit(solution)/shard_map/all_to_all | solution.py:385
  239.9 27.1 %all_to_all.42 = f32[32,64,128]{2,1,0:T(8,128)S(1)} all-to-all(f32[32,64,128]{2,1,0:T(8,128)S(1)} %get-tuple-element.31), channel_id=1, replica_groups=mesh['pix'=8,'tm'=4] {'pix','tm'}, dimensions={0} | all-to-all | bytes 2097152 | tf_op jit(solution)/shard_map/all_to_all | solution.py:385
  270.4 29.3 %all_to_all.43.rx = f32[32,64,128]{2,1,0:T(8,128)S(1)} all-to-all(f32[32,64,128]{2,1,0:T(8,128)S(1)} %bitcast.21), channel_id=1, replica_groups=mesh['pix'=8,'tm'=4] {'pix','tm'}, dimensions={0} | all-to-all | bytes 2097152 | tf_op jit(solution)/shard_map/all_to_all | solution.py:385
  305.4 29.5 %all_to_all.44 = f32[32,64,128]{2,1,0:T(8,128)S(1)} all-to-all(f32[32,64,128]{2,1,0:T(8,128)} %copy-done.8), channel_id=1, replica_groups=mesh['pix'=8,'tm'=4] {'pix','tm'}, dimensions={0} | all-to-all | bytes 2097152 | tf_op jit(solution)/shard_map/all_to_all | solution.py:385
  336.7 5.0 %collective-permute-start.7 = (f32[2,2,256,128]{3,2,1,0:T(8,128)S(1)}, f32[2,2,256,128]{3,2,1,0:T(8,128)S(1)}, u32[]{:S(2)}, u32[]{:S(2)}) collective-permute-start(f32[2,2,256,128]{3,2,1,0:T(8,128)S(1)} %shard_map.75.refs_1_), channel_id=1, source_target_pairs={{0,1},{1,2},{2,3},{4,5},{5,6},{6,7},{8,9},{9,10},{10,11},{12,13},{... | collective-permute-start | bytes 1572872 | tf_op jit(solution)/shard_map/ppermute | solution.py:315
  344.9 4.6 %collective-permute-start.6 = (f32[2,2,256,128]{3,2,1,0:T(8,128)S(1)}, f32[2,2,256,128]{3,2,1,0:T(8,128)S(1)}, u32[]{:S(2)}, u32[]{:S(2)}) collective-permute-start(f32[2,2,256,128]{3,2,1,0:T(8,128)S(1)} %shard_map.74.refs_0_), channel_id=1, source_target_pairs={{0,1},{1,2},{2,3},{4,5},{5,6},{6,7},{8,9},{9,10},{10,11},{12,13},{... | collective-permute-start | bytes 1572872 | tf_op jit(solution)/shard_map/ppermute | solution.py:315
  354.0 4.4 %collective-permute-start.9 = (f32[2,2,256,128]{3,2,1,0:T(8,128)S(1)}, f32[2,2,256,128]{3,2,1,0:T(8,128)S(1)}, u32[]{:S(2)}, u32[]{:S(2)}) collective-permute-start(f32[2,2,256,128]{3,2,1,0:T(8,128)S(1)} %collective-permute-done.7.refs_3_), channel_id=1, source_target_pairs={{0,1},{1,2},{2,3},{4,5},{5,6},{6,7},{8,9},{9,10},{10,11},{12,13},{... | collective-permute-start | bytes 1572872 | tf_op jit(solution)/shard_map/ppermute | solution.py:315
  359.8 5.5 %collective-permute-done.6.refs_2_ = f32[2,2,256,128]{3,2,1,0:T(8,128)S(1)} collective-permute-done((f32[2,2,256,128]{3,2,1,0:T(8,128)S(1)}, f32[2,2,256,128]{3,2,1,0:T(8,128)S(1)}, u32[]{:S(2)}, u32[]{:S(2)}) %collective-permute-start.6) | collective-permute-done | bytes 524320 | tf_op jit(solution)/shard_map/ppermute | solution.py:315
  371.0 5.5 %collective-permute-done.9.refs_5_ = f32[2,2,256,128]{3,2,1,0:T(8,128)S(1)} collective-permute-done((f32[2,2,256,128]{3,2,1,0:T(8,128)S(1)}, f32[2,2,256,128]{3,2,1,0:T(8,128)S(1)}, u32[]{:S(2)}, u32[]{:S(2)}) %collective-permute-start.9) | collective-permute-done | bytes 524320 | tf_op jit(solution)/shard_map/ppermute | solution.py:315
  382.2 5.5 %collective-permute-done.8.refs_4_ = f32[2,2,256,128]{3,2,1,0:T(8,128)S(1)} collective-permute-done((f32[2,2,256,128]{3,2,1,0:T(8,128)S(1)}, f32[2,2,256,128]{3,2,1,0:T(8,128)S(1)}, u32[]{:S(2)}, u32[]{:S(2)}) %collective-permute-start.8) | collective-permute-done | bytes 524320 | tf_op jit(solution)/shard_map/ppermute | solution.py:315
  399.0 4.4 %collective-permute-done.17.refs_3_ = f32[2,2,256,128]{3,2,1,0:T(8,128)S(1)} collective-permute-done((f32[2,2,256,128]{3,2,1,0:T(8,128)S(1)}, f32[2,2,256,128]{3,2,1,0:T(8,128)S(1)}, u32[]{:S(2)}, u32[]{:S(2)}) %collective-permute-start.17) | collective-permute-done | bytes 524320 | tf_op jit(solution)/shard_map/ppermute | solution.py:316
  415.7 6.4 %shard_map.76 = f32[96,128,128]{2,1,0:T(8,128)} custom-call(f32[8,96,16,128]{3,2,1,0:T(8,128)S(1)} %bitcast.18), custom_call_target="tpu_custom_call" | custom-call | tf_op jit(solution)/shard_map/pallas_call | solution.py:494
  (94 shorter events, 92.4 us)
Async XLA Ops:
  18.7 22.0 %all-to-all-start = ((f32[8,296,128]{2,1,0:T(8,128)}), f32[8,296,128]{2,1,0:T(8,128)S(1)}, u32[]{:S(2)}, u32[]{:S(2)}) async-start(f32[8,296,128]{2,1,0:T(8,128)} %get-tuple-element.21), calls=%async_computation | async-start | bytes 2424832 | tf_op jit(solution)/shard_map/all_to_all | solution.py:385
  70.9 18.9 %all-to-all-start.2 = ((f32[8,256,128]{2,1,0:T(8,128)}), f32[8,256,128]{2,1,0:T(8,128)S(1)}, u32[]{:S(2)}, u32[]{:S(2)}) async-start(f32[8,256,128]{2,1,0:T(8,128)} %shard_map.70), calls=%async_computation.2 | async-start | bytes 2097152 | tf_op jit(solution)/shard_map/all_to_all | solution.py:385
  95.2 92.8 %all-to-all-start.3 = ((f32[32,64,128]{2,1,0:T(8,128)}), f32[32,64,128]{2,1,0:T(8,128)S(1)}, u32[]{:S(2)}, u32[]{:S(2)}) async-start(f32[32,64,128]{2,1,0:T(8,128)} %get-tuple-element.25), calls=%async_computation.3 | async-start | bytes 2097152 | tf_op jit(solution)/shard_map/all_to_all | solution.py:385
  99.3 313.7 %all-gather.3.cloned.1.call-start = ((), (), s32[]{:S(2)}) async-start(), calls=%async_computation.8 | async-start | bytes 7077888 | tf_op jit(solution)/shard_map/all_gather | solution.py:493
  101.8 30.8 %collective-permute-start = (f32[4,256,128]{2,1,0:T(8,128)S(1)}, f32[4,256,128]{2,1,0:T(8,128)S(1)}, u32[]{:S(2)}, u32[]{:S(2)}) collective-permute-start(f32[4,256,128]{2,1,0:T(8,128)S(1)} %get-tuple-element.46), channel_id=1, source_target_pairs={{0,1},{1,2},{2,3},{3,0},{4,5},{5,6},{6,7},{7,4},{8,9},{9,10},{10,1... | collective-permute-start | bytes 1572872 | tf_op jit(solution)/shard_map/ppermute | solution.py:391
  103.5 67.4 %collective-permute-start.1 = (f32[4,256,128]{2,1,0:T(8,128)}, f32[4,256,128]{2,1,0:T(8,128)S(1)}, u32[]{:S(2)}, u32[]{:S(2)}) collective-permute-start(f32[4,256,128]{2,1,0:T(8,128)} %get-tuple-element.45), channel_id=1, source_target_pairs={{0,2},{1,3},{2,0},{3,1},{4,6},{5,7},{6,4},{7,5},{8,10},{9,11},{10,... | collective-permute-start | bytes 1572872 | tf_op jit(solution)/shard_map/ppermute | solution.py:391
  106.0 65.8 %collective-permute-start.2 = (f32[4,256,128]{2,1,0:T(8,128)}, f32[4,256,128]{2,1,0:T(8,128)}, u32[]{:S(2)}, u32[]{:S(2)}) collective-permute-start(f32[4,256,128]{2,1,0:T(8,128)} %get-tuple-element.44), channel_id=1, source_target_pairs={{0,3},{1,0},{2,1},{3,2},{4,7},{5,4},{6,5},{7,6},{8,11},{9,8},{10,9... | collective-permute-start | bytes 1572872 | tf_op jit(solution)/shard_map/ppermute | solution.py:391
  108.3 63.5 %collective-permute-start.3 = (f32[8,4,16,128]{3,2,1,0:T(8,128)}, f32[8,4,16,128]{3,2,1,0:T(8,128)}, u32[]{:S(2)}, u32[]{:S(2)}) collective-permute-start(f32[8,4,16,128]{3,2,1,0:T(8,128)} %get-tuple-element.42), channel_id=1, source_target_pairs={{0,1},{1,2},{2,3},{3,0},{4,5},{5,6},{6,7},{7,4},{8,9},{9,10},{10,1... | collective-permute-start | bytes 786440 | tf_op jit(solution)/shard_map/ppermute | solution.py:444
  108.9 79.0 %collective-permute-start.4 = (f32[8,4,16,128]{3,2,1,0:T(8,128)}, f32[8,4,16,128]{3,2,1,0:T(8,128)}, u32[]{:S(2)}, u32[]{:S(2)}) collective-permute-start(f32[8,4,16,128]{3,2,1,0:T(8,128)} %get-tuple-element.41), channel_id=1, source_target_pairs={{0,2},{1,3},{2,0},{3,1},{4,6},{5,7},{6,4},{7,5},{8,10},{9,11},{10,... | collective-permute-start | bytes 786440 | tf_op jit(solution)/shard_map/ppermute | solution.py:444
  132.6 55.3 %copy-start.10 = (f32[4,256,128]{2,1,0:T(8,128)}, f32[4,256,128]{2,1,0:T(8,128)S(1)}, u32[]{:S(2)}) copy-start(f32[4,256,128]{2,1,0:T(8,128)S(1)} %collective-permute-done.refs_1_) | copy-start | bytes 1572868
  132.6 55.3 %collective-permute-start.5 = (f32[8,4,16,128]{3,2,1,0:T(8,128)}, f32[8,4,16,128]{3,2,1,0:T(8,128)}, u32[]{:S(2)}, u32[]{:S(2)}) collective-permute-start(f32[8,4,16,128]{3,2,1,0:T(8,128)} %get-tuple-element.40), channel_id=1, source_target_pairs={{0,3},{1,0},{2,1},{3,2},{4,7},{5,4},{6,5},{7,6},{8,11},{9,8},{10,9... | collective-permute-start | bytes 786440 | tf_op jit(solution)/shard_map/ppermute | solution.py:444
  198.4 68.7 %copy-start.3 = (f32[4,512,128]{2,1,0:T(8,128)}, f32[4,512,128]{2,1,0:T(8,128)S(1)}, u32[]{:S(2)}) copy-start(f32[4,512,128]{2,1,0:T(8,128)S(1)} %get-tuple-element.33.told) | copy-start | bytes 3145732
  336.7 17.3 %collective-permute-start.7 = (f32[2,2,256,128]{3,2,1,0:T(8,128)S(1)}, f32[2,2,256,128]{3,2,1,0:T(8,128)S(1)}, u32[]{:S(2)}, u32[]{:S(2)}) collective-permute-start(f32[2,2,256,128]{3,2,1,0:T(8,128)S(1)} %shard_map.75.refs_1_), channel_id=1, source_target_pairs={{0,1},{1,2},{2,3},{4,5},{5,6},{6,7},{8,9},{9,10},{10,11},{12,13},{... | collective-permute-start | bytes 1572872 | tf_op jit(solution)/shard_map/ppermute | solution.py:315
  341.8 16.7 %collective-permute-start.11 = (f32[2,2,256,128]{3,2,1,0:T(8,128)S(1)}, f32[2,2,256,128]{3,2,1,0:T(8,128)S(1)}, u32[]{:S(2)}, u32[]{:S(2)}) collective-permute-start(f32[2,2,256,128]{3,2,1,0:T(8,128)S(1)} %shard_map.75.refs_1_), channel_id=1, source_target_pairs={{1,0},{2,1},{3,2},{5,4},{6,5},{7,6},{9,8},{10,9},{11,10},{13,12},{... | collective-permute-start | bytes 1572872 | tf_op jit(solution)/shard_map/ppermute | solution.py:316
  344.9 20.4 %collective-permute-start.6 = (f32[2,2,256,128]{3,2,1,0:T(8,128)S(1)}, f32[2,2,256,128]{3,2,1,0:T(8,128)S(1)}, u32[]{:S(2)}, u32[]{:S(2)}) collective-permute-start(f32[2,2,256,128]{3,2,1,0:T(8,128)S(1)} %shard_map.74.refs_0_), channel_id=1, source_target_pairs={{0,1},{1,2},{2,3},{4,5},{5,6},{6,7},{8,9},{9,10},{10,11},{12,13},{... | collective-permute-start | bytes 1572872 | tf_op jit(solution)/shard_map/ppermute | solution.py:315
  349.4 20.3 %collective-permute-start.10 = (f32[2,2,256,128]{3,2,1,0:T(8,128)S(1)}, f32[2,2,256,128]{3,2,1,0:T(8,128)S(1)}, u32[]{:S(2)}, u32[]{:S(2)}) collective-permute-start(f32[2,2,256,128]{3,2,1,0:T(8,128)S(1)} %shard_map.74.refs_0_), channel_id=1, source_target_pairs={{1,0},{2,1},{3,2},{5,4},{6,5},{7,6},{9,8},{10,9},{11,10},{13,12},{... | collective-permute-start | bytes 1572872 | tf_op jit(solution)/shard_map/ppermute | solution.py:316
  354.0 22.5 %collective-permute-start.9 = (f32[2,2,256,128]{3,2,1,0:T(8,128)S(1)}, f32[2,2,256,128]{3,2,1,0:T(8,128)S(1)}, u32[]{:S(2)}, u32[]{:S(2)}) collective-permute-start(f32[2,2,256,128]{3,2,1,0:T(8,128)S(1)} %collective-permute-done.7.refs_3_), channel_id=1, source_target_pairs={{0,1},{1,2},{2,3},{4,5},{5,6},{6,7},{8,9},{9,10},{10,11},{12,13},{... | collective-permute-start | bytes 1572872 | tf_op jit(solution)/shard_map/ppermute | solution.py:315
  358.5 22.5 %collective-permute-start.13 = (f32[2,2,256,128]{3,2,1,0:T(8,128)S(1)}, f32[2,2,256,128]{3,2,1,0:T(8,128)S(1)}, u32[]{:S(2)}, u32[]{:S(2)}) collective-permute-start(f32[2,2,256,128]{3,2,1,0:T(8,128)S(1)} %collective-permute-done.11.refs_7_), channel_id=1, source_target_pairs={{1,0},{2,1},{3,2},{5,4},{6,5},{7,6},{9,8},{10,9},{11,10},{13,12},{... | collective-permute-start | bytes 1572872 | tf_op jit(solution)/shard_map/ppermute | solution.py:316
  365.3 22.5 %collective-permute-start.8 = (f32[2,2,256,128]{3,2,1,0:T(8,128)S(1)}, f32[2,2,256,128]{3,2,1,0:T(8,128)S(1)}, u32[]{:S(2)}, u32[]{:S(2)}) collective-permute-start(f32[2,2,256,128]{3,2,1,0:T(8,128)S(1)} %collective-permute-done.6.refs_2_), channel_id=1, source_target_pairs={{0,1},{1,2},{2,3},{4,5},{5,6},{6,7},{8,9},{9,10},{10,11},{12,13},{... | collective-permute-start | bytes 1572872 | tf_op jit(solution)/shard_map/ppermute | solution.py:315
  369.7 22.5 %collective-permute-start.12 = (f32[2,2,256,128]{3,2,1,0:T(8,128)S(1)}, f32[2,2,256,128]{3,2,1,0:T(8,128)S(1)}, u32[]{:S(2)}, u32[]{:S(2)}) collective-permute-start(f32[2,2,256,128]{3,2,1,0:T(8,128)S(1)} %collective-permute-done.10.refs_6_), channel_id=1, source_target_pairs={{1,0},{2,1},{3,2},{5,4},{6,5},{7,6},{9,8},{10,9},{11,10},{13,12},{... | collective-permute-start | bytes 1572872 | tf_op jit(solution)/shard_map/ppermute | solution.py:316
  376.5 22.5 %collective-permute-start.15 = (f32[2,2,256,128]{3,2,1,0:T(8,128)S(1)}, f32[2,2,256,128]{3,2,1,0:T(8,128)S(1)}, u32[]{:S(2)}, u32[]{:S(2)}) collective-permute-start(f32[2,2,256,128]{3,2,1,0:T(8,128)S(1)} %collective-permute-done.9.refs_5_), channel_id=1, source_target_pairs={{0,1},{1,2},{2,3},{4,5},{5,6},{6,7},{8,9},{9,10},{10,11},{12,13},{... | collective-permute-start | bytes 1572872 | tf_op jit(solution)/shard_map/ppermute | solution.py:315
  380.9 22.5 %collective-permute-start.17 = (f32[2,2,256,128]{3,2,1,0:T(8,128)S(1)}, f32[2,2,256,128]{3,2,1,0:T(8,128)S(1)}, u32[]{:S(2)}, u32[]{:S(2)}) collective-permute-start(f32[2,2,256,128]{3,2,1,0:T(8,128)S(1)} %collective-permute-done.13.refs_9_), channel_id=1, source_target_pairs={{1,0},{2,1},{3,2},{5,4},{6,5},{7,6},{9,8},{10,9},{11,10},{13,12},{... | collective-permute-start | bytes 1572872 | tf_op jit(solution)/shard_map/ppermute | solution.py:316
  387.7 20.0 %collective-permute-start.14 = (f32[2,2,256,128]{3,2,1,0:T(8,128)S(1)}, f32[2,2,256,128]{3,2,1,0:T(8,128)S(1)}, u32[]{:S(2)}, u32[]{:S(2)}) collective-permute-start(f32[2,2,256,128]{3,2,1,0:T(8,128)S(1)} %collective-permute-done.8.refs_4_), channel_id=1, source_target_pairs={{0,1},{1,2},{2,3},{4,5},{5,6},{6,7},{8,9},{9,10},{10,11},{12,13},{... | collective-permute-start | bytes 1572872 | tf_op jit(solution)/shard_map/ppermute | solution.py:315
  392.2 19.8 %collective-permute-start.16 = (f32[2,2,256,128]{3,2,1,0:T(8,128)S(1)}, f32[2,2,256,128]{3,2,1,0:T(8,128)S(1)}, u32[]{:S(2)}, u32[]{:S(2)}) collective-permute-start(f32[2,2,256,128]{3,2,1,0:T(8,128)S(1)} %collective-permute-done.12.refs_8_), channel_id=1, source_target_pairs={{1,0},{2,1},{3,2},{5,4},{6,5},{7,6},{9,8},{10,9},{11,10},{13,12},{... | collective-permute-start | bytes 1572872 | tf_op jit(solution)/shard_map/ppermute | solution.py:316
  (19 other events, 193.2 us)
Sparse Core Ops, SparseCore 0:
  305.5 52.1 all-gather.2

commit v3 on v2

--- a/solution.py
+++ b/solution.py
@@ -245,10 +245,39 @@
         foot_out[o, 1] = n1
 
 
-def flip_kernel(rx, out):
-    npix, count, own, kb = rx.shape
+def flip_kernel(*refs, origins):
+    pieces, out, frames = refs[:-2], refs[-2], refs[-1]
+    count, own, _ = pieces[0].shape
+    places = [pl.multiple_of(o * own, SUBLANES) for o in origins(lax.axis_index("pix"))]
     for j in range(count):
-        out[j] = rx[:, j].reshape(npix * own, kb).T
+        for piece, place in zip(pieces, places):
+            frames[j, pl.ds(place, own), :] = piece[j]
+        out[j] = frames[j].T
+
+
+def pair_gather(x, axis, n):
+    chips = n // 2
+    power = chips & (chips - 1) == 0
+
+    def source(chip, s):
+        return chip ^ s if power else lax.rem(chip + s, chips)
+
+    def target(chip, s):
+        return chip ^ s if power else (chip - s) % chips
+
+    pieces = []
+    for s in range(chips):
+        perm = [(j, target(j // 2, s) * 2 + j % 2) for j in range(n)]
+        pieces.append(lax.ppermute(x, axis, perm) if s else x)
+    swap = [(j, j ^ 1) for j in range(n)]
+    for s in range(chips):
+        pieces.append(lax.ppermute(pieces[s], axis, swap))
+
+    def origins(me):
+        chip, core = me // 2, lax.rem(me, 2)
+        return [source(chip, s) * 2 + c for c in (core, 1 - core) for s in range(chips)]
+
+    return pieces, origins
 
 
 def early_kernel(*refs, n, count, axis):
@@ -490,14 +519,14 @@
     ]
     footprints_out = line_gather(chunks, "tm", ntm)
 
-    gathered = lax.all_gather(final, "pix", axis=0)
+    pieces, origins = pair_gather(final, "pix", npix)
     traces_out = kernel(
         flip_kernel, (blocks // several,),
-        [pl.BlockSpec((npix, several, own, kb), lambda j: (0, j, 0, 0))],
+        [pl.BlockSpec((several, own, kb), lambda j: (j, 0, 0))] * npix,
         pl.BlockSpec((several, kb, frames), lambda j: (j, 0, 0)),
         array(blocks, kb, frames),
-        limit=LIMIT,
-    )(gathered)
+        scratch=[pltpu.VMEM((several, frames, kb), f32)], limit=LIMIT, origins=origins,
+    )(*pieces)
     return footprints_out, traces_out
 
 

time: 431 us -> 434 us (level)
  starting transfers between devices: 54.7 us -> 93.5 us
  blocking collectives: 143 us -> 108 us
  between operations: 14.4 us -> 1.23 us
  waiting for transfers between devices: 133 us -> 142 us
    ppermute x0 -> x7, waiting for transfers between devices: none -> 44.6 us  [the longest x3 44.6 us: pair_gather(): pieces.append(lax.ppermute(x, axis, perm) if s else x)]
    all_to_all x5 -> x4, blocking collectives: 143 us -> 108 us  [exchange(): return lax.all_to_all(x, axes, 0, 0, tiled=True)]
    ppermute x6, starting transfers between devices: 7.09 us -> 38.3 us  [local(): lax.ppermute(piece, 'tm', [(j, (j + s) % ntm) for j in range(ntm)])]
    ppermute x6, waiting for transfers between devices: 76 us -> 49.9 us  [local(): lax.ppermute(piece, 'tm', [(j, (j + s) % ntm) for j in range(ntm)])]
    ppermute x6, waiting for transfers between devices: 28 us -> 1.92 us  [line_gather(): left[c] = lax.ppermute(left[c], axis, [(j, j + 1) for j in range(n - 1)])]
    ppermute x6, waiting for transfers between devices: 8.61 us -> 25.3 us  [line_gather(): right[c] = lax.ppermute(right[c], axis, [(j, j - 1) for j in range(1, n)])]
    all_to_all x3 -> x4, starting transfers between devices: 12.5 us -> 17.1 us  [exchange(): return lax.all_to_all(x, axes, 0, 0, tiled=True)]
    all_to_all x3 -> x4, waiting for transfers between devices: 19.8 us -> 19.8 us  [exchange(): return lax.all_to_all(x, axes, 0, 0, tiled=True)]
  transfers between devices with their start and end apart: 22 -> 29, of which waited for: 13 -> 17; matrix products, arithmetic and copies ran while one was open for 1% -> 1% of each run, Pallas kernels for 4% -> 6%
where the time goes in v3:
time: 434 us; the launch traced here: 432 us
  waiting for transfers between devices  142 us (33%)
  blocking collectives  108 us (25%)
  starting transfers between devices  93.5 us (22%)
  Pallas kernels  68.3 us (16%)
  local copies, waits for them, and re-layouts  17.3 us (4%)
    all_to_all x4, blocking collectives, exchange(): return lax.all_to_all(x, axes, 0, 0, tiled=True)  108 us
    ppermute x6, waiting for transfers between devices, local(): lax.ppermute(piece, 'tm', [(j, (j + s) % ntm) for j in range(ntm)])  49.9 us
    ppermute x3, waiting for transfers between devices, pair_gather(): pieces.append(lax.ppermute(x, axis, perm) if s else x)  44.6 us
    ppermute x6, starting transfers between devices, local(): lax.ppermute(piece, 'tm', [(j, (j + s) % ntm) for j in range(ntm)])  38.3 us
    ppermute x6, starting transfers between devices, line_gather(): left[c] = lax.ppermute(left[c], axis, [(j, j + 1) for j in range(n - 1)])  26.8 us
    ppermute x6, waiting for transfers between devices, line_gather(): right[c] = lax.ppermute(right[c], axis, [(j, j - 1) for j in range(1, n)])  25.3 us
    all_to_all x4, waiting for transfers between devices, exchange(): return lax.all_to_all(x, axes, 0, 0, tiled=True)  19.8 us
    all_to_all x4, starting transfers between devices, exchange(): return lax.all_to_all(x, axes, 0, 0, tiled=True)  17.1 us
  transfers between devices with their start and end apart: 29, of which 17 were waited for; matrix products, arithmetic and copies ran while one was open for 1% of the time, Pallas kernels for 6%

profile of v3, /device:TPU:0, one launch (start us, length us, event | category | flops | bytes accessed | tf_op | source)
XLA Modules:
  0.0 431.9 jit_solution(8702882230410239624)
XLA Ops:
  2.0 10.2 %shard_map.68 = (f32[16,256,128]{2,1,0:T(8,128)}, f32[8,296,128]{2,1,0:T(8,128)}) custom-call(s32[16,2]{1,0:T(8,128)} %copy.9.bl, bf16[16,256,128]{2,1,0:T(8,128)(2,1)} %y.1, f32[16,2,256,128]{3,2,1,0:T(8,128)} %foot.3, f32[96,128,128]{2,1,0:T(8,128)} %refs_7_.5, f32[96,128,128]{2,1,0:T(8,128)} %refs_7_.5, f32[96,128,128]{2,1,0:T(8,128)} %refs_7_.5, ...), custom_call_target="tpu_custom_call" | custom-call | tf_op jit(solution)/shard_map/pallas_call | solution.py:433
  12.2 4.9 %all-to-all-start = ((f32[8,296,128]{2,1,0:T(8,128)}), f32[8,296,128]{2,1,0:T(8,128)S(1)}, u32[]{:S(2)}, u32[]{:S(2)}) async-start(f32[8,296,128]{2,1,0:T(8,128)} %get-tuple-element.21), calls=%async_computation | async-start | bytes 2424832 | tf_op jit(solution)/shard_map/all_to_all | solution.py:414
  17.1 5.8 %shard_map.69.before = f32[48,16,128]{2,1,0:T(8,128)} custom-call(s32[96]{0:T(128)} %order.11, s32[1]{0:T(128)} %bitcast.pix, f32[96,128,128]{2,1,0:T(8,128)} %refs_7_.5, f32[96,128,128]{2,1,0:T(8,128)} %refs_7_.5, f32[96,128,128]{2,1,0:T(8,128)} %refs_7_.5, f32[96,128,128]{2,1,0:T(8,128)} %refs_7_.5, f32[96,128,128]{2,1,0:T(8,128)} %refs_7_.5, ...), custom_call_target="tpu_custom_call" | custom-call | tf_op jit(solution)/shard_map/pallas_call | solution.py:451
  23.8 10.4 %all-to-all-done.rx = f32[8,296,128]{2,1,0:T(8,128)S(1)} async-done(((f32[8,296,128]{2,1,0:T(8,128)}), f32[8,296,128]{2,1,0:T(8,128)S(1)}, u32[]{:S(2)}, u32[]{:S(2)}) %all-to-all-start) | async-done | bytes 1212448 | tf_op jit(solution)/shard_map/all_to_all | solution.py:414
  38.0 18.5 %all_to_all.40 = f32[8,256,128]{2,1,0:T(8,128)} all-to-all(f32[8,256,128]{2,1,0:T(8,128)S(1)} %get-tuple-element.22), channel_id=1, replica_groups=mesh['pix'=8,'tm'=4] {'pix'}, dimensions={0} | all-to-all | bytes 2097152 | tf_op jit(solution)/shard_map/all_to_all | solution.py:414
  56.5 7.9 %shard_map.70 = f32[8,256,128]{2,1,0:T(8,128)} custom-call(f32[16,256,128]{2,1,0:T(8,128)} %get-tuple-element.23.base, f32[16,2,256,128]{3,2,1,0:T(8,128)} %foot.3, f32[8,16,16,128]{3,2,1,0:T(8,128)} %bitcast.21), custom_call_target="tpu_custom_call" | custom-call | tf_op jit(solution)/shard_map/pallas_call | solution.py:475
  68.0 5.8 %shard_map.71.before = f32[48,16,128]{2,1,0:T(8,128)} custom-call(s32[96]{0:T(128)} %order.11, s32[1]{0:T(128)} %bitcast.pix, f32[96,128,128]{2,1,0:T(8,128)} %refs_7_.5, f32[96,128,128]{2,1,0:T(8,128)} %refs_7_.5, f32[96,128,128]{2,1,0:T(8,128)} %refs_7_.5, f32[96,128,128]{2,1,0:T(8,128)} %refs_7_.5, f32[96,128,128]{2,1,0:T(8,128)} %refs_7_.5, ...), custom_call_target="tpu_custom_call" | custom-call | tf_op jit(solution)/shard_map/pallas_call | solution.py:451
  73.8 9.5 %all-to-all-done.2.rx = f32[8,256,128]{2,1,0:T(8,128)S(1)} async-done(((f32[8,256,128]{2,1,0:T(8,128)}), f32[8,256,128]{2,1,0:T(8,128)S(1)}, u32[]{:S(2)}, u32[]{:S(2)}) %all-to-all-start.2) | async-done | bytes 1048608 | tf_op jit(solution)/shard_map/all_to_all | solution.py:414
  104.8 19.5 %collective-permute-done.2.refs_3_ = f32[4,256,128]{2,1,0:T(8,128)S(1)} collective-permute-done((f32[4,256,128]{2,1,0:T(8,128)S(1)}, f32[4,256,128]{2,1,0:T(8,128)S(1)}, u32[]{:S(2)}, u32[]{:S(2)}) %collective-permute-start.2) | collective-permute-done | bytes 524320 | tf_op jit(solution)/shard_map/ppermute | solution.py:420
  124.2 29.7 %collective-permute-start.3 = (f32[8,4,16,128]{3,2,1,0:T(8,128)}, f32[8,4,16,128]{3,2,1,0:T(8,128)}, u32[]{:S(2)}, u32[]{:S(2)}) collective-permute-start(f32[8,4,16,128]{3,2,1,0:T(8,128)} %get-tuple-element.42), channel_id=1, source_target_pairs={{0,1},{1,2},{2,3},{3,0},{4,5},{5,6},{6,7},{7,4},{8,9},{9,10},{10,1... | collective-permute-start | bytes 786440 | tf_op jit(solution)/shard_map/ppermute | solution.py:473
  155.2 20.5 %collective-permute-done.1.refs_2_ = f32[4,256,128]{2,1,0:T(8,128)S(1)} collective-permute-done((f32[4,256,128]{2,1,0:T(8,128)}, f32[4,256,128]{2,1,0:T(8,128)S(1)}, u32[]{:S(2)}, u32[]{:S(2)}) %collective-permute-start.1) | collective-permute-done | bytes 524320 | tf_op jit(solution)/shard_map/ppermute | solution.py:420
  176.5 10.0 %collective-permute-done.4.refs_6_ = f32[8,4,16,128]{3,2,1,0:T(8,128)} collective-permute-done((f32[8,4,16,128]{3,2,1,0:T(8,128)}, f32[8,4,16,128]{3,2,1,0:T(8,128)}, u32[]{:S(2)}, u32[]{:S(2)}) %collective-permute-start.4) | collective-permute-done | bytes 262176 | tf_op jit(solution)/shard_map/ppermute | solution.py:473
  189.6 7.3 %shard_map.72 = (f32[4,256,512]{2,1,0:T(8,128)S(1)}, f32[4,2,256,128]{3,2,1,0:T(8,128)S(1)}, f32[4,512,128]{2,1,0:T(8,128)S(1)}, f32[4,512,128]{2,1,0:T(8,128)S(1)}, f32[8,4,72,128]{3,2,1,0:T(8,128)S(1)}) custom-call(f32[4,256,128]{2,1,0:T(8,128)S(1)} %copy-done.4, f32[4,256,128]{2,1,0:T(8,128)} %collective-permute-done.refs_1_, ...), custom_call_target="tpu_custom_call" | custom-call | tf_op jit(solution)/shard_map/pallas_call | solution.py:400
  196.9 32.8 %all_to_all.41.rx = f32[32,72,128]{2,1,0:T(8,128)S(1)} all-to-all(f32[32,72,128]{2,1,0:T(8,128)S(1)} %bitcast.19), channel_id=1, replica_groups=mesh['pix'=8,'tm'=4] {'pix','tm'}, dimensions={0} | all-to-all | bytes 2359296 | tf_op jit(solution)/shard_map/all_to_all | solution.py:414
  232.6 27.1 %all_to_all.42 = f32[32,64,128]{2,1,0:T(8,128)S(1)} all-to-all(f32[32,64,128]{2,1,0:T(8,128)S(1)} %get-tuple-element.31), channel_id=1, replica_groups=mesh['pix'=8,'tm'=4] {'pix','tm'}, dimensions={0} | all-to-all | bytes 2097152 | tf_op jit(solution)/shard_map/all_to_all | solution.py:414
  263.0 29.3 %all_to_all.43.rx = f32[32,64,128]{2,1,0:T(8,128)S(1)} all-to-all(f32[32,64,128]{2,1,0:T(8,128)S(1)} %bitcast.20), channel_id=1, replica_groups=mesh['pix'=8,'tm'=4] {'pix','tm'}, dimensions={0} | all-to-all | bytes 2097152 | tf_op jit(solution)/shard_map/all_to_all | solution.py:414
  306.1 29.7 %collective-permute-done.20.refs_3_ = f32[96,16,128]{2,1,0:T(8,128)} collective-permute-done((f32[96,16,128]{2,1,0:T(8,128)}, f32[96,16,128]{2,1,0:T(8,128)}, u32[]{:S(2)}, u32[]{:S(2)}) %collective-permute-start.20) | collective-permute-done | bytes 786464 | tf_op jit(solution)/shard_map/ppermute | solution.py:271
  335.9 14.9 %collective-permute-done.19.refs_2_ = f32[96,16,128]{2,1,0:T(8,128)} collective-permute-done((f32[96,16,128]{2,1,0:T(8,128)}, f32[96,16,128]{2,1,0:T(8,128)}, u32[]{:S(2)}, u32[]{:S(2)}) %collective-permute-start.19) | collective-permute-done | bytes 786464 | tf_op jit(solution)/shard_map/ppermute | solution.py:271
  358.5 4.6 %collective-permute-start.6 = (f32[2,2,256,128]{3,2,1,0:T(8,128)S(1)}, f32[2,2,256,128]{3,2,1,0:T(8,128)S(1)}, u32[]{:S(2)}, u32[]{:S(2)}) collective-permute-start(f32[2,2,256,128]{3,2,1,0:T(8,128)S(1)} %shard_map.74.refs_0_), channel_id=1, source_target_pairs={{0,1},{1,2},{2,3},{4,5},{5,6},{6,7},{8,9},{9,10},{10,11},{12,13},{... | collective-permute-start | bytes 1572872 | tf_op jit(solution)/shard_map/ppermute | solution.py:344
  369.0 4.9 %collective-permute-done.10.refs_6_ = f32[2,2,256,128]{3,2,1,0:T(8,128)S(1)} collective-permute-done((f32[2,2,256,128]{3,2,1,0:T(8,128)S(1)}, f32[2,2,256,128]{3,2,1,0:T(8,128)S(1)}, u32[]{:S(2)}, u32[]{:S(2)}) %collective-permute-start.10) | collective-permute-done | bytes 524320 | tf_op jit(solution)/shard_map/ppermute | solution.py:345
  379.8 5.3 %collective-permute-done.11.refs_7_ = f32[2,2,256,128]{3,2,1,0:T(8,128)S(1)} collective-permute-done((f32[2,2,256,128]{3,2,1,0:T(8,128)S(1)}, f32[2,2,256,128]{3,2,1,0:T(8,128)S(1)}, u32[]{:S(2)}, u32[]{:S(2)}) %collective-permute-start.11) | collective-permute-done | bytes 524320 | tf_op jit(solution)/shard_map/ppermute | solution.py:345
  391.1 5.3 %collective-permute-done.12.refs_8_ = f32[2,2,256,128]{3,2,1,0:T(8,128)S(1)} collective-permute-done((f32[2,2,256,128]{3,2,1,0:T(8,128)S(1)}, f32[2,2,256,128]{3,2,1,0:T(8,128)S(1)}, u32[]{:S(2)}, u32[]{:S(2)}) %collective-permute-start.12) | collective-permute-done | bytes 524320 | tf_op jit(solution)/shard_map/ppermute | solution.py:345
  402.3 5.3 %collective-permute-done.13.refs_9_ = f32[2,2,256,128]{3,2,1,0:T(8,128)S(1)} collective-permute-done((f32[2,2,256,128]{3,2,1,0:T(8,128)S(1)}, f32[2,2,256,128]{3,2,1,0:T(8,128)S(1)}, u32[]{:S(2)}, u32[]{:S(2)}) %collective-permute-start.13) | collective-permute-done | bytes 524320 | tf_op jit(solution)/shard_map/ppermute | solution.py:345
  413.5 9.9 %shard_map.76 = f32[96,128,128]{2,1,0:T(8,128)} custom-call(f32[96,16,128]{2,1,0:T(8,128)S(1)} %copy-done.9, f32[96,16,128]{2,1,0:T(8,128)} %collective-permute-done.18.refs_1_, f32[96,16,128]{2,1,0:T(8,128)} %collective-permute-done.19.refs_2_, f32[96,16,128]{2,1,0:T(8,128)} %collective-permute-done.20.refs_3_, ...), custom_call_target="tpu_custom_call" | custom-call | tf_op jit(solution)/shard_map/pallas_call | solution.py:523
  (106 shorter events, 101.7 us)
Async XLA Ops:
  12.2 22.0 %all-to-all-start = ((f32[8,296,128]{2,1,0:T(8,128)}), f32[8,296,128]{2,1,0:T(8,128)S(1)}, u32[]{:S(2)}, u32[]{:S(2)}) async-start(f32[8,296,128]{2,1,0:T(8,128)} %get-tuple-element.21), calls=%async_computation | async-start | bytes 2424832 | tf_op jit(solution)/shard_map/all_to_all | solution.py:414
  88.7 97.8 %all-to-all-start.3 = ((f32[32,64,128]{2,1,0:T(8,128)}), f32[32,64,128]{2,1,0:T(8,128)S(1)}, u32[]{:S(2)}, u32[]{:S(2)}) async-start(f32[32,64,128]{2,1,0:T(8,128)} %get-tuple-element.25), calls=%async_computation.3 | async-start | bytes 2097152 | tf_op jit(solution)/shard_map/all_to_all | solution.py:414
  95.3 29.0 %collective-permute-start.2 = (f32[4,256,128]{2,1,0:T(8,128)S(1)}, f32[4,256,128]{2,1,0:T(8,128)S(1)}, u32[]{:S(2)}, u32[]{:S(2)}) collective-permute-start(f32[4,256,128]{2,1,0:T(8,128)S(1)} %get-tuple-element.44), channel_id=1, source_target_pairs={{0,3},{1,0},{2,1},{3,2},{4,7},{5,4},{6,5},{7,6},{8,11},{9,8},{10,9... | collective-permute-start | bytes 1572872 | tf_op jit(solution)/shard_map/ppermute | solution.py:420
  98.9 76.8 %collective-permute-start.1 = (f32[4,256,128]{2,1,0:T(8,128)}, f32[4,256,128]{2,1,0:T(8,128)S(1)}, u32[]{:S(2)}, u32[]{:S(2)}) collective-permute-start(f32[4,256,128]{2,1,0:T(8,128)} %get-tuple-element.45), channel_id=1, source_target_pairs={{0,2},{1,3},{2,0},{3,1},{4,6},{5,7},{6,4},{7,5},{8,10},{9,11},{10,... | collective-permute-start | bytes 1572872 | tf_op jit(solution)/shard_map/ppermute | solution.py:420
  98.9 77.6 %collective-permute-start = (f32[4,256,128]{2,1,0:T(8,128)}, f32[4,256,128]{2,1,0:T(8,128)}, u32[]{:S(2)}, u32[]{:S(2)}) collective-permute-start(f32[4,256,128]{2,1,0:T(8,128)} %get-tuple-element.46), channel_id=1, source_target_pairs={{0,1},{1,2},{2,3},{3,0},{4,5},{5,6},{6,7},{7,4},{8,9},{9,10},{10,1... | collective-permute-start | bytes 1572872 | tf_op jit(solution)/shard_map/ppermute | solution.py:420
  100.9 75.6 %collective-permute-start.5 = (f32[8,4,16,128]{3,2,1,0:T(8,128)}, f32[8,4,16,128]{3,2,1,0:T(8,128)}, u32[]{:S(2)}, u32[]{:S(2)}) collective-permute-start(f32[8,4,16,128]{3,2,1,0:T(8,128)} %get-tuple-element.40), channel_id=1, source_target_pairs={{0,3},{1,0},{2,1},{3,2},{4,7},{5,4},{6,5},{7,6},{8,11},{9,8},{10,9... | collective-permute-start | bytes 786440 | tf_op jit(solution)/shard_map/ppermute | solution.py:473
  103.6 82.8 %collective-permute-start.4 = (f32[8,4,16,128]{3,2,1,0:T(8,128)}, f32[8,4,16,128]{3,2,1,0:T(8,128)}, u32[]{:S(2)}, u32[]{:S(2)}) collective-permute-start(f32[8,4,16,128]{3,2,1,0:T(8,128)} %get-tuple-element.41), channel_id=1, source_target_pairs={{0,2},{1,3},{2,0},{3,1},{4,6},{5,7},{6,4},{7,5},{8,10},{9,11},{10,... | collective-permute-start | bytes 786440 | tf_op jit(solution)/shard_map/ppermute | solution.py:473
  124.2 62.2 %collective-permute-start.3 = (f32[8,4,16,128]{3,2,1,0:T(8,128)}, f32[8,4,16,128]{3,2,1,0:T(8,128)}, u32[]{:S(2)}, u32[]{:S(2)}) collective-permute-start(f32[8,4,16,128]{3,2,1,0:T(8,128)} %get-tuple-element.42), channel_id=1, source_target_pairs={{0,1},{1,2},{2,3},{3,0},{4,5},{5,6},{6,7},{7,4},{8,9},{9,10},{10,1... | collective-permute-start | bytes 786440 | tf_op jit(solution)/shard_map/ppermute | solution.py:473
  298.0 52.8 %all-to-all-start.7 = ((f32[32,64,128]{2,1,0:T(8,128)}), f32[32,64,128]{2,1,0:T(8,128)S(1)}, u32[]{:S(2)}, u32[]{:S(2)}) async-start(f32[32,64,128]{2,1,0:T(8,128)} %copy-done.7), calls=%async_computation.7 | async-start | bytes 2097152 | tf_op jit(solution)/shard_map/all_to_all | solution.py:414
  302.6 33.3 %collective-permute-start.20 = (f32[96,16,128]{2,1,0:T(8,128)}, f32[96,16,128]{2,1,0:T(8,128)}, u32[]{:S(2)}, u32[]{:S(2)}) collective-permute-start(f32[96,16,128]{2,1,0:T(8,128)} %copy-done.8), channel_id=1, source_target_pairs={{0,24},{4,28},{8,16},{12,20},{16,8},{20,12},{24,0},{28,4},{1,25},{... | collective-permute-start | bytes 2359304 | tf_op jit(solution)/shard_map/ppermute | solution.py:271
  305.3 45.5 %collective-permute-start.19 = (f32[96,16,128]{2,1,0:T(8,128)}, f32[96,16,128]{2,1,0:T(8,128)}, u32[]{:S(2)}, u32[]{:S(2)}) collective-permute-start(f32[96,16,128]{2,1,0:T(8,128)} %copy-done.8), channel_id=1, source_target_pairs={{0,16},{4,20},{8,24},{12,28},{16,0},{20,4},{24,8},{28,12},{1,17},{... | collective-permute-start | bytes 2359304 | tf_op jit(solution)/shard_map/ppermute | solution.py:271
  305.9 52.6 %collective-permute-start.21 = (f32[96,16,128]{2,1,0:T(8,128)}, f32[96,16,128]{2,1,0:T(8,128)}, u32[]{:S(2)}, u32[]{:S(2)}) collective-permute-start(f32[96,16,128]{2,1,0:T(8,128)} %copy-done.8), channel_id=1, source_target_pairs={{0,4},{4,0},{8,12},{12,8},{16,20},{20,16},{24,28},{28,24},{1,5},{5... | collective-permute-start | bytes 2359304 | tf_op jit(solution)/shard_map/ppermute | solution.py:274
  305.9 57.2 %collective-permute-start.18 = (f32[96,16,128]{2,1,0:T(8,128)}, f32[96,16,128]{2,1,0:T(8,128)}, u32[]{:S(2)}, u32[]{:S(2)}) collective-permute-start(f32[96,16,128]{2,1,0:T(8,128)} %copy-done.8), channel_id=1, source_target_pairs={{0,8},{4,12},{8,0},{12,4},{16,24},{20,28},{24,16},{28,20},{1,9},{5... | collective-permute-start | bytes 2359304 | tf_op jit(solution)/shard_map/ppermute | solution.py:271
  335.9 28.6 %collective-permute-start.24 = (f32[96,16,128]{2,1,0:T(8,128)}, f32[96,16,128]{2,1,0:T(8,128)}, u32[]{:S(2)}, u32[]{:S(2)}) collective-permute-start(f32[96,16,128]{2,1,0:T(8,128)} %collective-permute-done.20.refs_3_), channel_id=1, source_target_pairs={{0,4},{4,0},{8,12},{12,8},{16,20},{20,16},{24,28},{28,24},{1,5},{5... | collective-permute-start | bytes 2359304 | tf_op jit(solution)/shard_map/ppermute | solution.py:274
  350.8 40.2 %collective-permute-start.23 = (f32[96,16,128]{2,1,0:T(8,128)}, f32[96,16,128]{2,1,0:T(8,128)}, u32[]{:S(2)}, u32[]{:S(2)}) collective-permute-start(f32[96,16,128]{2,1,0:T(8,128)} %collective-permute-done.19.refs_2_), channel_id=1, source_target_pairs={{0,4},{4,0},{8,12},{12,8},{16,20},{20,16},{24,28},{28,24},{1,5},{5... | collective-permute-start | bytes 2359304 | tf_op jit(solution)/shard_map/ppermute | solution.py:274
  363.1 22.0 %collective-permute-start.11 = (f32[2,2,256,128]{3,2,1,0:T(8,128)S(1)}, f32[2,2,256,128]{3,2,1,0:T(8,128)S(1)}, u32[]{:S(2)}, u32[]{:S(2)}) collective-permute-start(f32[2,2,256,128]{3,2,1,0:T(8,128)S(1)} %shard_map.75.refs_1_), channel_id=1, source_target_pairs={{1,0},{2,1},{3,2},{5,4},{6,5},{7,6},{9,8},{10,9},{11,10},{13,12},{... | collective-permute-start | bytes 1572872 | tf_op jit(solution)/shard_map/ppermute | solution.py:345
  364.4 22.2 %collective-permute-start.7 = (f32[2,2,256,128]{3,2,1,0:T(8,128)S(1)}, f32[2,2,256,128]{3,2,1,0:T(8,128)S(1)}, u32[]{:S(2)}, u32[]{:S(2)}) collective-permute-start(f32[2,2,256,128]{3,2,1,0:T(8,128)S(1)} %shard_map.75.refs_1_), channel_id=1, source_target_pairs={{0,1},{1,2},{2,3},{4,5},{5,6},{6,7},{8,9},{9,10},{10,11},{12,13},{... | collective-permute-start | bytes 1572872 | tf_op jit(solution)/shard_map/ppermute | solution.py:344
  373.9 22.5 %collective-permute-start.12 = (f32[2,2,256,128]{3,2,1,0:T(8,128)S(1)}, f32[2,2,256,128]{3,2,1,0:T(8,128)S(1)}, u32[]{:S(2)}, u32[]{:S(2)}) collective-permute-start(f32[2,2,256,128]{3,2,1,0:T(8,128)S(1)} %collective-permute-done.10.refs_6_), channel_id=1, source_target_pairs={{1,0},{2,1},{3,2},{5,4},{6,5},{7,6},{9,8},{10,9},{11,10},{13,12},{... | collective-permute-start | bytes 1572872 | tf_op jit(solution)/shard_map/ppermute | solution.py:345
  375.4 22.5 %collective-permute-start.8 = (f32[2,2,256,128]{3,2,1,0:T(8,128)S(1)}, f32[2,2,256,128]{3,2,1,0:T(8,128)S(1)}, u32[]{:S(2)}, u32[]{:S(2)}) collective-permute-start(f32[2,2,256,128]{3,2,1,0:T(8,128)S(1)} %collective-permute-done.6.refs_2_), channel_id=1, source_target_pairs={{0,1},{1,2},{2,3},{4,5},{5,6},{6,7},{8,9},{9,10},{10,11},{12,13},{... | collective-permute-start | bytes 1572872 | tf_op jit(solution)/shard_map/ppermute | solution.py:344
  385.1 22.5 %collective-permute-start.13 = (f32[2,2,256,128]{3,2,1,0:T(8,128)S(1)}, f32[2,2,256,128]{3,2,1,0:T(8,128)S(1)}, u32[]{:S(2)}, u32[]{:S(2)}) collective-permute-start(f32[2,2,256,128]{3,2,1,0:T(8,128)S(1)} %collective-permute-done.11.refs_7_), channel_id=1, source_target_pairs={{1,0},{2,1},{3,2},{5,4},{6,5},{7,6},{9,8},{10,9},{11,10},{13,12},{... | collective-permute-start | bytes 1572872 | tf_op jit(solution)/shard_map/ppermute | solution.py:345
  386.6 22.5 %collective-permute-start.9 = (f32[2,2,256,128]{3,2,1,0:T(8,128)S(1)}, f32[2,2,256,128]{3,2,1,0:T(8,128)S(1)}, u32[]{:S(2)}, u32[]{:S(2)}) collective-permute-start(f32[2,2,256,128]{3,2,1,0:T(8,128)S(1)} %collective-permute-done.7.refs_3_), channel_id=1, source_target_pairs={{0,1},{1,2},{2,3},{4,5},{5,6},{6,7},{8,9},{9,10},{10,11},{12,13},{... | collective-permute-start | bytes 1572872 | tf_op jit(solution)/shard_map/ppermute | solution.py:344
  391.0 22.5 %collective-permute-start.22 = (f32[96,16,128]{2,1,0:T(8,128)}, f32[96,16,128]{2,1,0:T(8,128)S(1)}, u32[]{:S(2)}, u32[]{:S(2)}) collective-permute-start(f32[96,16,128]{2,1,0:T(8,128)} %collective-permute-done.18.refs_1_), channel_id=1, source_target_pairs={{0,4},{4,0},{8,12},{12,8},{16,20},{20,16},{24,28},{28,24},{1,5},{5... | collective-permute-start | bytes 2359304 | tf_op jit(solution)/shard_map/ppermute | solution.py:274
  396.4 28.8 %collective-permute-start.16 = (f32[2,2,256,128]{3,2,1,0:T(8,128)S(1)}, f32[2,2,256,128]{3,2,1,0:T(8,128)S(1)}, u32[]{:S(2)}, u32[]{:S(2)}) collective-permute-start(f32[2,2,256,128]{3,2,1,0:T(8,128)S(1)} %collective-permute-done.12.refs_8_), channel_id=1, source_target_pairs={{1,0},{2,1},{3,2},{5,4},{6,5},{7,6},{9,8},{10,9},{11,10},{13,12},{... | collective-permute-start | bytes 1572872 | tf_op jit(solution)/shard_map/ppermute | solution.py:345
  397.8 27.3 %collective-permute-start.14 = (f32[2,2,256,128]{3,2,1,0:T(8,128)S(1)}, f32[2,2,256,128]{3,2,1,0:T(8,128)S(1)}, u32[]{:S(2)}, u32[]{:S(2)}) collective-permute-start(f32[2,2,256,128]{3,2,1,0:T(8,128)S(1)} %collective-permute-done.8.refs_4_), channel_id=1, source_target_pairs={{0,1},{1,2},{2,3},{4,5},{5,6},{6,7},{8,9},{9,10},{10,11},{12,13},{... | collective-permute-start | bytes 1572872 | tf_op jit(solution)/shard_map/ppermute | solution.py:344
  (26 other events, 400.9 us)

commit v4 on v3

--- a/solution.py
+++ b/solution.py
@@ -62,14 +62,16 @@
     at = pl.program_id(0) * step
     count = bl.shape[0]
     kb = foot.shape[3]
-    for i in range(step):
-        f0, f1 = split(foot[i, 0]), split(foot[i, 1])
-        base = y[i].astype(f32) - rows_by_columns(f1, split(t1s[i][0]))
-        base_out[i] = base
-        residual = base - rows_by_columns(f0, split(t0s[i][0]))
-        terms = rows_by_columns(split(residual), f0, 0)
+    some = range(step)
+    f0 = [split(foot[i, 0]) for i in some]
+    f1 = [split(foot[i, 1]) for i in some]
+    base = [y[i].astype(f32) - rows_by_columns(f1[i], split(t1s[i][0])) for i in some]
+    residual = [split(base[i] - rows_by_columns(f0[i], split(t0s[i][0]))) for i in some]
+    terms = [rows_by_columns(residual[i], f0[i], 0) for i in some]
+    for i in some:
+        base_out[i] = base[i]
         p = at + i
-        pay[:, pl.ds(pl.multiple_of(p * own, SUBLANES), own), :] = terms.reshape(parts, own, kb)
+        pay[:, pl.ds(pl.multiple_of(p * own, SUBLANES), own), :] = terms[i].reshape(parts, own, kb)
         for g in range(2):
             norm = jnp.broadcast_to(squares(foot[i, g])[None], (parts, 1, kb))
             pay[:, pl.ds(count * own + g * count + p, 1), :] = norm
@@ -88,12 +90,12 @@
 def second_kernel(base, foot, rx, pay, *, parts, own, step):
     at = pl.program_id(0) * step
     kb = foot.shape[3]
-    for i in range(step):
-        f0, f1 = split(foot[i, 0]), split(foot[i, 1])
-        trace = rx[:, i].reshape(parts * own, kb)
-        residual = base[i] - rows_by_rows(f0, split(trace))
-        terms = rows_by_columns(split(residual), f1, 0)
-        pay[:, pl.ds(pl.multiple_of((at + i) * own, SUBLANES), own), :] = terms.reshape(parts, own, kb)
+    some = range(step)
+    traces = [split(rx[:, i].reshape(parts * own, kb)) for i in some]
+    residual = [split(base[i] - rows_by_rows(split(foot[i, 0]), traces[i])) for i in some]
+    terms = [rows_by_columns(residual[i], split(foot[i, 1]), 0) for i in some]
+    for i in some:
+        pay[:, pl.ds(pl.multiple_of((at + i) * own, SUBLANES), own), :] = terms[i].reshape(parts, own, kb)
 
 
 def prepare_kernel(order, pix, *refs, own, step):
@@ -108,8 +110,6 @@
         after, back, norms1, totals, norms = refs
         norms1[...] = jnp.zeros(norms1.shape, f32)
         norms[...] = jnp.zeros(norms.shape, f32)
-    elif other == "final":
-        norms, after0, after, back, final, totals = refs
     else:
         norms, after, back, totals = refs
     sources = rx.shape[0]
@@ -139,12 +139,14 @@
             j = place[listing[s * outper + i, group]] - group * bpg
             back[s, i * own:(i + 1) * own, :] = after[j]
 
-    if other == "final":
-
-        @pl.loop(0, bpg, unroll=4)
-        def _(j):
-            final[order[j]] = after0[j]
-            final[order[bpg + j]] = after[j]
+
+def sort_kernel(order, after0, after1, final):
+    bpg = after0.shape[0]
+
+    @pl.loop(0, bpg, unroll=4)
+    def _(j):
+        final[order[j]] = after0[j]
+        final[order[bpg + j]] = after1[j]
 
 
 def owner(tables, rx, before, extra, *, group, per, outs, outper, other):
@@ -153,8 +155,6 @@
     shapes = [before.shape, (outs, outper * own, kb)]
     if other == "norms":
         shapes.append(norms_shape)
-    if other == "final":
-        shapes.append((2 * bpg, own, kb))
     scratch = [pltpu.VMEM(before.shape, f32)]
     if other == "norms":
         scratch.append(pltpu.VMEM(norms_shape, f32))
@@ -187,13 +187,19 @@
 
 
 def footprint_phase(residual, f0, f1, t0, t1):
-    kb = f0.shape[1]
-    scale0 = kb * squares(t0) + EPSILON
-    scale1 = kb * squares(t1) + EPSILON
-    s0, s1 = split(t0), split(t1)
-    n0 = jnp.maximum(f0 + rows_by_columns(split(residual), s0) / scale0, 0.0)
-    residual = residual - rows_by_rows(split(n0 - f0), s0)
-    n1 = jnp.maximum(f1 + rows_by_columns(split(residual), s1) / scale1, 0.0)
+    kb = f0[0].shape[1]
+    s0, s1 = [split(t) for t in t0], [split(t) for t in t1]
+
+    def renewed(residual, foot, trace, parts):
+        weights = [rows_by_columns(split(r), s) for r, s in zip(residual, parts)]
+        return [
+            jnp.maximum(f + w / (kb * squares(t) + EPSILON), 0.0)
+            for f, w, t in zip(foot, weights, trace)
+        ]
+
+    n0 = renewed(residual, f0, t0, s0)
+    residual = [r - rows_by_rows(split(n - f), s) for r, n, f, s in zip(residual, n0, f0, s0)]
+    n1 = renewed(residual, f1, t1, s1)
     return residual, n0, n1, s1
 
 
@@ -203,24 +209,33 @@
     me = lax.axis_index("tm")
     count, kb = foot.shape[0], foot.shape[3]
     own = (pay.shape[2] - up8(2 * count)) // count
-    for i in range(count):
-        f0, f1 = foot[i, 0], foot[i, 1]
-        y = jnp.concatenate([ref[i] for ref in ys], axis=1)
-        t0 = jnp.concatenate([ref[:, i].reshape(ref.shape[0] * ref.shape[2], kb) for ref in t0s], axis=0)
-        t1 = incoming(rx1, i, me, ntm)
-        residual = y - rows_by_rows(split(f0), split(t0)) - rows_by_rows(split(f1), split(t1))
+    pair = divisor(count, (2, 1))
+    for at in range(0, count, pair):
+        some = range(at, at + pair)
+        f0 = [foot[i, 0] for i in some]
+        f1 = [foot[i, 1] for i in some]
+        y = [jnp.concatenate([ref[i] for ref in ys], axis=1) for i in some]
+        t0 = [
+            jnp.concatenate([ref[:, i].reshape(ref.shape[0] * ref.shape[2], kb) for ref in t0s], axis=0)
+            for i in some
+        ]
+        t1 = [incoming(rx1, i, me, ntm) for i in some]
+        residual = [r - rows_by_rows(split(f), split(t)) for r, f, t in zip(y, f0, t0)]
+        residual = [r - rows_by_rows(split(f), split(t)) for r, f, t in zip(residual, f1, t1)]
         residual, n0, n1, s1 = footprint_phase(residual, f0, f1, t0, t1)
-        residual = residual - rows_by_rows(split(n1 - f1), s1)
-        residual_out[i] = residual
-        foot_out[i, 0] = n0
-        foot_out[i, 1] = n1
-        t0_out[i] = t0
-        t1_out[i] = t1
-        outgoing(pay, rows_by_columns(split(residual), split(n0), 0), i, me, ntm)
-        for g, new in enumerate((n0, n1)):
-            norm = jnp.broadcast_to(squares(new)[None, None], pay.shape[:2] + (1, kb))
-            row = count * own + g * count + i
-            pay[:, :, row:row + 1, :] = norm
+        residual = [r - rows_by_rows(split(n - f), s) for r, n, f, s in zip(residual, n1, f1, s1)]
+        terms = [rows_by_columns(split(r), split(n), 0) for r, n in zip(residual, n0)]
+        for o, i in enumerate(some):
+            residual_out[i] = residual[o]
+            foot_out[i, 0] = n0[o]
+            foot_out[i, 1] = n1[o]
+            t0_out[i] = t0[o]
+            t1_out[i] = t1[o]
+            outgoing(pay, terms[o], i, me, ntm)
+            for g, new in enumerate((n0[o], n1[o])):
+                norm = jnp.broadcast_to(squares(new)[None, None], pay.shape[:2] + (1, kb))
+                row = count * own + g * count + i
+                pay[:, :, row:row + 1, :] = norm
 
 
 def fourth_kernel(residual_in, foot, told, rx, residual_out, pay, *, ntm):
@@ -234,15 +249,18 @@
 
 def last_kernel(residual_in, foot, told, rx0, rx1, foot_out, *, ntm, skip):
     me = lax.axis_index("tm")
+    some = range(skip, skip + foot_out.shape[0])
+    f0 = [foot[i, 0] for i in some]
+    f1 = [foot[i, 1] for i in some]
+    t0 = [incoming(rx0, i, me, ntm) for i in some]
+    t1 = [incoming(rx1, i, me, ntm) for i in some]
+    residual = [
+        residual_in[i] - rows_by_rows(split(f), split(t - told[i])) for i, f, t in zip(some, f1, t1)
+    ]
+    _, n0, n1, _ = footprint_phase(residual, f0, f1, t0, t1)
     for o in range(foot_out.shape[0]):
-        i = skip + o
-        f0, f1 = foot[i, 0], foot[i, 1]
-        t0 = incoming(rx0, i, me, ntm)
-        t1 = incoming(rx1, i, me, ntm)
-        residual = residual_in[i] - rows_by_rows(split(f1), split(t1 - told[i]))
-        _, n0, n1, _ = footprint_phase(residual, f0, f1, t0, t1)
-        foot_out[o, 0] = n0
-        foot_out[o, 1] = n1
+        foot_out[o, 0] = n0[o]
+        foot_out[o, 1] = n1[o]
 
 
 def flip_kernel(*refs, origins):
@@ -506,8 +524,8 @@
     rx0 = landed(spread(back))
     residual, pay = resident(fourth_kernel, [residual_type, array(*narrow)], ntm=ntm)(residual, foot, t0_old, rx0)
     got = spread(pay)
-    after1, back, final = owner(
-        tables, got, after1, (norms1, after0), group=1, per=share, outs=everyone, outper=share, other="final"
+    after1, back = owner(
+        tables, got, after1, (norms1,), group=1, per=share, outs=everyone, outper=share, other=None
     )
     rx1 = landed(spread(back))
 
@@ -519,6 +537,14 @@
     ]
     footprints_out = line_gather(chunks, "tm", ntm)
 
+    final = pl.pallas_call(
+        sort_kernel,
+        in_specs=[whole(pltpu.SMEM), whole(pltpu.VMEM), whole(pltpu.VMEM)],
+        out_specs=whole(pltpu.VMEM),
+        out_shape=array(blocks, own, kb),
+        compiler_params=pltpu.CompilerParams(vmem_limit_bytes=LIMIT),
+        name="sort",
+    )(block_order, after0, after1)
     pieces, origins = pair_gather(final, "pix", npix)
     traces_out = kernel(
         flip_kernel, (blocks // several,),

time: 434 us -> 428 us (0.986)
  Pallas kernels: 68.3 us -> 62.2 us
    unnamed x45 -> x49, local copies, waits for them, and re-layouts: 14.1 us -> 16.7 us
  transfers between devices with their start and end apart: 29 -> 29, of which waited for: 17 -> 17; matrix products, arithmetic and copies ran while one was open for 1% -> 1% of each run, Pallas kernels for 6% -> 7%
where the time goes in v4:
time: 428 us; the launch traced here: 425 us
  waiting for transfers between devices  138 us (32%)
  blocking collectives  108 us (25%)
  starting transfers between devices  93.9 us (22%)
  Pallas kernels  62.2 us (15%)
  local copies, waits for them, and re-layouts  19.9 us (5%)
    all_to_all x4, blocking collectives, exchange(): return lax.all_to_all(x, axes, 0, 0, tiled=True)  108 us
    ppermute x6, waiting for transfers between devices, local(): lax.ppermute(piece, 'tm', [(j, (j + s) % ntm) for j in range(ntm)])  49.9 us
    ppermute x3, waiting for transfers between devices, pair_gather(): pieces.append(lax.ppermute(x, axis, perm) if s else x)  41 us
    ppermute x6, starting transfers between devices, local(): lax.ppermute(piece, 'tm', [(j, (j + s) % ntm) for j in range(ntm)])  38.3 us
    ppermute x6, starting transfers between devices, line_gather(): left[c] = lax.ppermute(left[c], axis, [(j, j + 1) for j in range(n - 1)])  27.1 us
    ppermute x6, waiting for transfers between devices, line_gather(): right[c] = lax.ppermute(right[c], axis, [(j, j - 1) for j in range(1, n)])  25.3 us
    all_to_all x4, waiting for transfers between devices, exchange(): return lax.all_to_all(x, axes, 0, 0, tiled=True)  19.8 us
    all_to_all x4, starting transfers between devices, exchange(): return lax.all_to_all(x, axes, 0, 0, tiled=True)  17.3 us
  transfers between devices with their start and end apart: 29, of which 17 were waited for; matrix products, arithmetic and copies ran while one was open for 1% of the time, Pallas kernels for 7%

profile of v4, /device:TPU:0, one launch (start us, length us, event | category | flops | bytes accessed | tf_op | source)
XLA Modules:
  0.0 425.4 jit_solution(16138082708587031712)
XLA Ops:
  2.0 8.1 %shard_map.68 = (f32[16,256,128]{2,1,0:T(8,128)}, f32[8,296,128]{2,1,0:T(8,128)}) custom-call(s32[16,2]{1,0:T(8,128)} %copy.9.bl, bf16[16,256,128]{2,1,0:T(8,128)(2,1)} %y.1, f32[16,2,256,128]{3,2,1,0:T(8,128)} %foot.3, f32[96,128,128]{2,1,0:T(8,128)} %refs_7_.5, f32[96,128,128]{2,1,0:T(8,128)} %refs_7_.5, f32[96,128,128]{2,1,0:T(8,128)} %refs_7_.5, ...), custom_call_target="tpu_custom_call" | custom-call | tf_op jit(solution)/shard_map/pallas_call | solution.py:451
  10.1 4.9 %all-to-all-start = ((f32[8,296,128]{2,1,0:T(8,128)}), f32[8,296,128]{2,1,0:T(8,128)S(1)}, u32[]{:S(2)}, u32[]{:S(2)}) async-start(f32[8,296,128]{2,1,0:T(8,128)} %get-tuple-element.21), calls=%async_computation | async-start | bytes 2424832 | tf_op jit(solution)/shard_map/all_to_all | solution.py:432
  15.0 5.8 %shard_map.69.before = f32[48,16,128]{2,1,0:T(8,128)} custom-call(s32[96]{0:T(128)} %order.13, s32[1]{0:T(128)} %bitcast.pix, f32[96,128,128]{2,1,0:T(8,128)} %refs_7_.5, f32[96,128,128]{2,1,0:T(8,128)} %refs_7_.5, f32[96,128,128]{2,1,0:T(8,128)} %refs_7_.5, f32[96,128,128]{2,1,0:T(8,128)} %refs_7_.5, f32[96,128,128]{2,1,0:T(8,128)} %refs_7_.5, ...), custom_call_target="tpu_custom_call" | custom-call | tf_op jit(solution)/shard_map/pallas_call | solution.py:469
  21.7 10.4 %all-to-all-done.rx = f32[8,296,128]{2,1,0:T(8,128)S(1)} async-done(((f32[8,296,128]{2,1,0:T(8,128)}), f32[8,296,128]{2,1,0:T(8,128)S(1)}, u32[]{:S(2)}, u32[]{:S(2)}) %all-to-all-start) | async-done | bytes 1212448 | tf_op jit(solution)/shard_map/all_to_all | solution.py:432
  35.9 18.4 %all_to_all.40 = f32[8,256,128]{2,1,0:T(8,128)} all-to-all(f32[8,256,128]{2,1,0:T(8,128)S(1)} %get-tuple-element.22), channel_id=1, replica_groups=mesh['pix'=8,'tm'=4] {'pix'}, dimensions={0} | all-to-all | bytes 2097152 | tf_op jit(solution)/shard_map/all_to_all | solution.py:432
  54.3 6.0 %shard_map.70 = f32[8,256,128]{2,1,0:T(8,128)} custom-call(f32[16,256,128]{2,1,0:T(8,128)} %get-tuple-element.23.base, f32[16,2,256,128]{3,2,1,0:T(8,128)} %foot.3, f32[8,16,16,128]{3,2,1,0:T(8,128)} %bitcast.21), custom_call_target="tpu_custom_call" | custom-call | tf_op jit(solution)/shard_map/pallas_call | solution.py:493
  63.9 5.8 %shard_map.71.before = f32[48,16,128]{2,1,0:T(8,128)} custom-call(s32[96]{0:T(128)} %order.13, s32[1]{0:T(128)} %bitcast.pix, f32[96,128,128]{2,1,0:T(8,128)} %refs_7_.5, f32[96,128,128]{2,1,0:T(8,128)} %refs_7_.5, f32[96,128,128]{2,1,0:T(8,128)} %refs_7_.5, f32[96,128,128]{2,1,0:T(8,128)} %refs_7_.5, f32[96,128,128]{2,1,0:T(8,128)} %refs_7_.5, ...), custom_call_target="tpu_custom_call" | custom-call | tf_op jit(solution)/shard_map/pallas_call | solution.py:469
  69.7 9.5 %all-to-all-done.2.rx = f32[8,256,128]{2,1,0:T(8,128)S(1)} async-done(((f32[8,256,128]{2,1,0:T(8,128)}), f32[8,256,128]{2,1,0:T(8,128)S(1)}, u32[]{:S(2)}, u32[]{:S(2)}) %all-to-all-start.2) | async-done | bytes 1048608 | tf_op jit(solution)/shard_map/all_to_all | solution.py:432
  100.7 19.5 %collective-permute-done.2.refs_3_ = f32[4,256,128]{2,1,0:T(8,128)S(1)} collective-permute-done((f32[4,256,128]{2,1,0:T(8,128)S(1)}, f32[4,256,128]{2,1,0:T(8,128)S(1)}, u32[]{:S(2)}, u32[]{:S(2)}) %collective-permute-start.2) | collective-permute-done | bytes 524320 | tf_op jit(solution)/shard_map/ppermute | solution.py:438
  120.2 29.7 %collective-permute-start.3 = (f32[8,4,16,128]{3,2,1,0:T(8,128)}, f32[8,4,16,128]{3,2,1,0:T(8,128)}, u32[]{:S(2)}, u32[]{:S(2)}) collective-permute-start(f32[8,4,16,128]{3,2,1,0:T(8,128)} %get-tuple-element.42), channel_id=1, source_target_pairs={{0,1},{1,2},{2,3},{3,0},{4,5},{5,6},{6,7},{7,4},{8,9},{9,10},{10,1... | collective-permute-start | bytes 786440 | tf_op jit(solution)/shard_map/ppermute | solution.py:491
  151.2 20.5 %collective-permute-done.1.refs_2_ = f32[4,256,128]{2,1,0:T(8,128)S(1)} collective-permute-done((f32[4,256,128]{2,1,0:T(8,128)}, f32[4,256,128]{2,1,0:T(8,128)S(1)}, u32[]{:S(2)}, u32[]{:S(2)}) %collective-permute-start.1) | collective-permute-done | bytes 524320 | tf_op jit(solution)/shard_map/ppermute | solution.py:438
  172.4 10.0 %collective-permute-done.4.refs_6_ = f32[8,4,16,128]{3,2,1,0:T(8,128)} collective-permute-done((f32[8,4,16,128]{3,2,1,0:T(8,128)}, f32[8,4,16,128]{3,2,1,0:T(8,128)}, u32[]{:S(2)}, u32[]{:S(2)}) %collective-permute-start.4) | collective-permute-done | bytes 262176 | tf_op jit(solution)/shard_map/ppermute | solution.py:491
  185.5 5.4 %shard_map.72 = (f32[4,256,512]{2,1,0:T(8,128)S(1)}, f32[4,2,256,128]{3,2,1,0:T(8,128)S(1)}, f32[4,512,128]{2,1,0:T(8,128)S(1)}, f32[4,512,128]{2,1,0:T(8,128)S(1)}, f32[8,4,72,128]{3,2,1,0:T(8,128)S(1)}) custom-call(f32[4,256,128]{2,1,0:T(8,128)S(1)} %copy-done.4, f32[4,256,128]{2,1,0:T(8,128)} %collective-permute-done.refs_1_, ...), custom_call_target="tpu_custom_call" | custom-call | tf_op jit(solution)/shard_map/pallas_call | solution.py:418
  191.0 32.8 %all_to_all.41.rx = f32[32,72,128]{2,1,0:T(8,128)S(1)} all-to-all(f32[32,72,128]{2,1,0:T(8,128)S(1)} %bitcast.19), channel_id=1, replica_groups=mesh['pix'=8,'tm'=4] {'pix','tm'}, dimensions={0} | all-to-all | bytes 2359296 | tf_op jit(solution)/shard_map/all_to_all | solution.py:432
  227.4 27.1 %all_to_all.42 = f32[32,64,128]{2,1,0:T(8,128)S(1)} all-to-all(f32[32,64,128]{2,1,0:T(8,128)S(1)} %get-tuple-element.31), channel_id=1, replica_groups=mesh['pix'=8,'tm'=4] {'pix','tm'}, dimensions={0} | all-to-all | bytes 2097152 | tf_op jit(solution)/shard_map/all_to_all | solution.py:432
  257.8 29.3 %all_to_all.43.rx = f32[32,64,128]{2,1,0:T(8,128)S(1)} all-to-all(f32[32,64,128]{2,1,0:T(8,128)S(1)} %bitcast.20), channel_id=1, replica_groups=mesh['pix'=8,'tm'=4] {'pix','tm'}, dimensions={0} | all-to-all | bytes 2097152 | tf_op jit(solution)/shard_map/all_to_all | solution.py:432
  303.6 25.7 %collective-permute-done.20.refs_3_ = f32[96,16,128]{2,1,0:T(8,128)} collective-permute-done((f32[96,16,128]{2,1,0:T(8,128)}, f32[96,16,128]{2,1,0:T(8,128)}, u32[]{:S(2)}, u32[]{:S(2)}) %collective-permute-start.20) | collective-permute-done | bytes 786464 | tf_op jit(solution)/shard_map/ppermute | solution.py:289
  329.4 15.3 %collective-permute-done.19.refs_2_ = f32[96,16,128]{2,1,0:T(8,128)} collective-permute-done((f32[96,16,128]{2,1,0:T(8,128)}, f32[96,16,128]{2,1,0:T(8,128)}, u32[]{:S(2)}, u32[]{:S(2)}) %collective-permute-start.19) | collective-permute-done | bytes 786464 | tf_op jit(solution)/shard_map/ppermute | solution.py:289
  351.5 4.9 %collective-permute-start.6 = (f32[2,2,256,128]{3,2,1,0:T(8,128)S(1)}, f32[2,2,256,128]{3,2,1,0:T(8,128)S(1)}, u32[]{:S(2)}, u32[]{:S(2)}) collective-permute-start(f32[2,2,256,128]{3,2,1,0:T(8,128)S(1)} %shard_map.74.refs_0_), channel_id=1, source_target_pairs={{0,1},{1,2},{2,3},{4,5},{5,6},{6,7},{8,9},{9,10},{10,11},{12,13},{... | collective-permute-start | bytes 1572872 | tf_op jit(solution)/shard_map/ppermute | solution.py:362
  362.3 4.9 %collective-permute-done.10.refs_6_ = f32[2,2,256,128]{3,2,1,0:T(8,128)S(1)} collective-permute-done((f32[2,2,256,128]{3,2,1,0:T(8,128)S(1)}, f32[2,2,256,128]{3,2,1,0:T(8,128)S(1)}, u32[]{:S(2)}, u32[]{:S(2)}) %collective-permute-start.10) | collective-permute-done | bytes 524320 | tf_op jit(solution)/shard_map/ppermute | solution.py:363
  373.1 5.3 %collective-permute-done.11.refs_7_ = f32[2,2,256,128]{3,2,1,0:T(8,128)S(1)} collective-permute-done((f32[2,2,256,128]{3,2,1,0:T(8,128)S(1)}, f32[2,2,256,128]{3,2,1,0:T(8,128)S(1)}, u32[]{:S(2)}, u32[]{:S(2)}) %collective-permute-start.11) | collective-permute-done | bytes 524320 | tf_op jit(solution)/shard_map/ppermute | solution.py:363
  384.4 5.3 %collective-permute-done.12.refs_8_ = f32[2,2,256,128]{3,2,1,0:T(8,128)S(1)} collective-permute-done((f32[2,2,256,128]{3,2,1,0:T(8,128)S(1)}, f32[2,2,256,128]{3,2,1,0:T(8,128)S(1)}, u32[]{:S(2)}, u32[]{:S(2)}) %collective-permute-start.12) | collective-permute-done | bytes 524320 | tf_op jit(solution)/shard_map/ppermute | solution.py:363
  395.5 5.3 %collective-permute-done.13.refs_9_ = f32[2,2,256,128]{3,2,1,0:T(8,128)S(1)} collective-permute-done((f32[2,2,256,128]{3,2,1,0:T(8,128)S(1)}, f32[2,2,256,128]{3,2,1,0:T(8,128)S(1)}, u32[]{:S(2)}, u32[]{:S(2)}) %collective-permute-start.13) | collective-permute-done | bytes 524320 | tf_op jit(solution)/shard_map/ppermute | solution.py:363
  406.8 10.0 %shard_map.76 = f32[96,128,128]{2,1,0:T(8,128)} custom-call(f32[96,16,128]{2,1,0:T(8,128)} %sort.1.refs_0_, f32[96,16,128]{2,1,0:T(8,128)} %collective-permute-done.18.refs_1_, f32[96,16,128]{2,1,0:T(8,128)} %collective-permute-done.19.refs_2_, f32[96,16,128]{2,1,0:T(8,128)} %collective-permute-done.20.refs_3_, ...), custom_call_target="tpu_custom_call" | custom-call | tf_op jit(solution)/shard_map/pallas_call | solution.py:549
  (111 shorter events, 104.3 us)
Async XLA Ops:
  10.1 22.0 %all-to-all-start = ((f32[8,296,128]{2,1,0:T(8,128)}), f32[8,296,128]{2,1,0:T(8,128)S(1)}, u32[]{:S(2)}, u32[]{:S(2)}) async-start(f32[8,296,128]{2,1,0:T(8,128)} %get-tuple-element.21), calls=%async_computation | async-start | bytes 2424832 | tf_op jit(solution)/shard_map/all_to_all | solution.py:432
  84.6 97.8 %all-to-all-start.3 = ((f32[32,64,128]{2,1,0:T(8,128)}), f32[32,64,128]{2,1,0:T(8,128)S(1)}, u32[]{:S(2)}, u32[]{:S(2)}) async-start(f32[32,64,128]{2,1,0:T(8,128)} %get-tuple-element.25), calls=%async_computation.3 | async-start | bytes 2097152 | tf_op jit(solution)/shard_map/all_to_all | solution.py:432
  91.2 29.0 %collective-permute-start.2 = (f32[4,256,128]{2,1,0:T(8,128)S(1)}, f32[4,256,128]{2,1,0:T(8,128)S(1)}, u32[]{:S(2)}, u32[]{:S(2)}) collective-permute-start(f32[4,256,128]{2,1,0:T(8,128)S(1)} %get-tuple-element.44), channel_id=1, source_target_pairs={{0,3},{1,0},{2,1},{3,2},{4,7},{5,4},{6,5},{7,6},{8,11},{9,8},{10,9... | collective-permute-start | bytes 1572872 | tf_op jit(solution)/shard_map/ppermute | solution.py:438
  94.8 76.8 %collective-permute-start.1 = (f32[4,256,128]{2,1,0:T(8,128)}, f32[4,256,128]{2,1,0:T(8,128)S(1)}, u32[]{:S(2)}, u32[]{:S(2)}) collective-permute-start(f32[4,256,128]{2,1,0:T(8,128)} %get-tuple-element.45), channel_id=1, source_target_pairs={{0,2},{1,3},{2,0},{3,1},{4,6},{5,7},{6,4},{7,5},{8,10},{9,11},{10,... | collective-permute-start | bytes 1572872 | tf_op jit(solution)/shard_map/ppermute | solution.py:438
  94.8 77.6 %collective-permute-start = (f32[4,256,128]{2,1,0:T(8,128)}, f32[4,256,128]{2,1,0:T(8,128)}, u32[]{:S(2)}, u32[]{:S(2)}) collective-permute-start(f32[4,256,128]{2,1,0:T(8,128)} %get-tuple-element.46), channel_id=1, source_target_pairs={{0,1},{1,2},{2,3},{3,0},{4,5},{5,6},{6,7},{7,4},{8,9},{9,10},{10,1... | collective-permute-start | bytes 1572872 | tf_op jit(solution)/shard_map/ppermute | solution.py:438
  96.8 75.6 %collective-permute-start.5 = (f32[8,4,16,128]{3,2,1,0:T(8,128)}, f32[8,4,16,128]{3,2,1,0:T(8,128)}, u32[]{:S(2)}, u32[]{:S(2)}) collective-permute-start(f32[8,4,16,128]{3,2,1,0:T(8,128)} %get-tuple-element.40), channel_id=1, source_target_pairs={{0,3},{1,0},{2,1},{3,2},{4,7},{5,4},{6,5},{7,6},{8,11},{9,8},{10,9... | collective-permute-start | bytes 786440 | tf_op jit(solution)/shard_map/ppermute | solution.py:491
  99.6 82.8 %collective-permute-start.4 = (f32[8,4,16,128]{3,2,1,0:T(8,128)}, f32[8,4,16,128]{3,2,1,0:T(8,128)}, u32[]{:S(2)}, u32[]{:S(2)}) collective-permute-start(f32[8,4,16,128]{3,2,1,0:T(8,128)} %get-tuple-element.41), channel_id=1, source_target_pairs={{0,2},{1,3},{2,0},{3,1},{4,6},{5,7},{6,4},{7,5},{8,10},{9,11},{10,... | collective-permute-start | bytes 786440 | tf_op jit(solution)/shard_map/ppermute | solution.py:491
  120.2 62.2 %collective-permute-start.3 = (f32[8,4,16,128]{3,2,1,0:T(8,128)}, f32[8,4,16,128]{3,2,1,0:T(8,128)}, u32[]{:S(2)}, u32[]{:S(2)}) collective-permute-start(f32[8,4,16,128]{3,2,1,0:T(8,128)} %get-tuple-element.42), channel_id=1, source_target_pairs={{0,1},{1,2},{2,3},{3,0},{4,5},{5,6},{6,7},{7,4},{8,9},{9,10},{10,1... | collective-permute-start | bytes 786440 | tf_op jit(solution)/shard_map/ppermute | solution.py:491
  291.8 52.9 %all-to-all-start.7 = ((f32[32,64,128]{2,1,0:T(8,128)}), f32[32,64,128]{2,1,0:T(8,128)S(1)}, u32[]{:S(2)}, u32[]{:S(2)}) async-start(f32[32,64,128]{2,1,0:T(8,128)} %copy-done.7), calls=%async_computation.7 | async-start | bytes 2097152 | tf_op jit(solution)/shard_map/all_to_all | solution.py:432
  300.1 29.2 %collective-permute-start.20 = (f32[96,16,128]{2,1,0:T(8,128)}, f32[96,16,128]{2,1,0:T(8,128)}, u32[]{:S(2)}, u32[]{:S(2)}) collective-permute-start(f32[96,16,128]{2,1,0:T(8,128)} %sort.1.refs_0_), channel_id=1, source_target_pairs={{0,24},{4,28},{8,16},{12,20},{16,8},{20,12},{24,0},{28,4},{1,25},{... | collective-permute-start | bytes 2359304 | tf_op jit(solution)/shard_map/ppermute | solution.py:289
  302.6 42.0 %collective-permute-start.19 = (f32[96,16,128]{2,1,0:T(8,128)}, f32[96,16,128]{2,1,0:T(8,128)}, u32[]{:S(2)}, u32[]{:S(2)}) collective-permute-start(f32[96,16,128]{2,1,0:T(8,128)} %sort.1.refs_0_), channel_id=1, source_target_pairs={{0,16},{4,20},{8,24},{12,28},{16,0},{20,4},{24,8},{28,12},{1,17},{... | collective-permute-start | bytes 2359304 | tf_op jit(solution)/shard_map/ppermute | solution.py:289
  303.2 48.3 %collective-permute-start.21 = (f32[96,16,128]{2,1,0:T(8,128)}, f32[96,16,128]{2,1,0:T(8,128)}, u32[]{:S(2)}, u32[]{:S(2)}) collective-permute-start(f32[96,16,128]{2,1,0:T(8,128)} %sort.1.refs_0_), channel_id=1, source_target_pairs={{0,4},{4,0},{8,12},{12,8},{16,20},{20,16},{24,28},{28,24},{1,5},{5... | collective-permute-start | bytes 2359304 | tf_op jit(solution)/shard_map/ppermute | solution.py:292
  303.2 53.2 %collective-permute-start.18 = (f32[96,16,128]{2,1,0:T(8,128)}, f32[96,16,128]{2,1,0:T(8,128)}, u32[]{:S(2)}, u32[]{:S(2)}) collective-permute-start(f32[96,16,128]{2,1,0:T(8,128)} %sort.1.refs_0_), channel_id=1, source_target_pairs={{0,8},{4,12},{8,0},{12,4},{16,24},{20,28},{24,16},{28,20},{1,9},{5... | collective-permute-start | bytes 2359304 | tf_op jit(solution)/shard_map/ppermute | solution.py:289
  329.4 28.3 %collective-permute-start.24 = (f32[96,16,128]{2,1,0:T(8,128)}, f32[96,16,128]{2,1,0:T(8,128)}, u32[]{:S(2)}, u32[]{:S(2)}) collective-permute-start(f32[96,16,128]{2,1,0:T(8,128)} %collective-permute-done.20.refs_3_), channel_id=1, source_target_pairs={{0,4},{4,0},{8,12},{12,8},{16,20},{20,16},{24,28},{28,24},{1,5},{5... | collective-permute-start | bytes 2359304 | tf_op jit(solution)/shard_map/ppermute | solution.py:292
  344.6 39.7 %collective-permute-start.23 = (f32[96,16,128]{2,1,0:T(8,128)}, f32[96,16,128]{2,1,0:T(8,128)}, u32[]{:S(2)}, u32[]{:S(2)}) collective-permute-start(f32[96,16,128]{2,1,0:T(8,128)} %collective-permute-done.19.refs_2_), channel_id=1, source_target_pairs={{0,4},{4,0},{8,12},{12,8},{16,20},{20,16},{24,28},{28,24},{1,5},{5... | collective-permute-start | bytes 2359304 | tf_op jit(solution)/shard_map/ppermute | solution.py:292
  357.7 22.2 %collective-permute-start.7 = (f32[2,2,256,128]{3,2,1,0:T(8,128)S(1)}, f32[2,2,256,128]{3,2,1,0:T(8,128)S(1)}, u32[]{:S(2)}, u32[]{:S(2)}) collective-permute-start(f32[2,2,256,128]{3,2,1,0:T(8,128)S(1)} %shard_map.75.refs_1_), channel_id=1, source_target_pairs={{0,1},{1,2},{2,3},{4,5},{5,6},{6,7},{8,9},{9,10},{10,11},{12,13},{... | collective-permute-start | bytes 1572872 | tf_op jit(solution)/shard_map/ppermute | solution.py:362
  367.2 22.5 %collective-permute-start.12 = (f32[2,2,256,128]{3,2,1,0:T(8,128)S(1)}, f32[2,2,256,128]{3,2,1,0:T(8,128)S(1)}, u32[]{:S(2)}, u32[]{:S(2)}) collective-permute-start(f32[2,2,256,128]{3,2,1,0:T(8,128)S(1)} %collective-permute-done.10.refs_6_), channel_id=1, source_target_pairs={{1,0},{2,1},{3,2},{5,4},{6,5},{7,6},{9,8},{10,9},{11,10},{13,12},{... | collective-permute-start | bytes 1572872 | tf_op jit(solution)/shard_map/ppermute | solution.py:363
  368.7 22.5 %collective-permute-start.8 = (f32[2,2,256,128]{3,2,1,0:T(8,128)S(1)}, f32[2,2,256,128]{3,2,1,0:T(8,128)S(1)}, u32[]{:S(2)}, u32[]{:S(2)}) collective-permute-start(f32[2,2,256,128]{3,2,1,0:T(8,128)S(1)} %collective-permute-done.6.refs_2_), channel_id=1, source_target_pairs={{0,1},{1,2},{2,3},{4,5},{5,6},{6,7},{8,9},{9,10},{10,11},{12,13},{... | collective-permute-start | bytes 1572872 | tf_op jit(solution)/shard_map/ppermute | solution.py:362
  378.4 22.5 %collective-permute-start.13 = (f32[2,2,256,128]{3,2,1,0:T(8,128)S(1)}, f32[2,2,256,128]{3,2,1,0:T(8,128)S(1)}, u32[]{:S(2)}, u32[]{:S(2)}) collective-permute-start(f32[2,2,256,128]{3,2,1,0:T(8,128)S(1)} %collective-permute-done.11.refs_7_), channel_id=1, source_target_pairs={{1,0},{2,1},{3,2},{5,4},{6,5},{7,6},{9,8},{10,9},{11,10},{13,12},{... | collective-permute-start | bytes 1572872 | tf_op jit(solution)/shard_map/ppermute | solution.py:363
  379.9 22.5 %collective-permute-start.9 = (f32[2,2,256,128]{3,2,1,0:T(8,128)S(1)}, f32[2,2,256,128]{3,2,1,0:T(8,128)S(1)}, u32[]{:S(2)}, u32[]{:S(2)}) collective-permute-start(f32[2,2,256,128]{3,2,1,0:T(8,128)S(1)} %collective-permute-done.7.refs_3_), channel_id=1, source_target_pairs={{0,1},{1,2},{2,3},{4,5},{5,6},{6,7},{8,9},{9,10},{10,11},{12,13},{... | collective-permute-start | bytes 1572872 | tf_op jit(solution)/shard_map/ppermute | solution.py:362
  384.3 22.5 %collective-permute-start.22 = (f32[96,16,128]{2,1,0:T(8,128)}, f32[96,16,128]{2,1,0:T(8,128)S(1)}, u32[]{:S(2)}, u32[]{:S(2)}) collective-permute-start(f32[96,16,128]{2,1,0:T(8,128)} %collective-permute-done.18.refs_1_), channel_id=1, source_target_pairs={{0,4},{4,0},{8,12},{12,8},{16,20},{20,16},{24,28},{28,24},{1,5},{5... | collective-permute-start | bytes 2359304 | tf_op jit(solution)/shard_map/ppermute | solution.py:292
  389.6 28.9 %collective-permute-start.16 = (f32[2,2,256,128]{3,2,1,0:T(8,128)S(1)}, f32[2,2,256,128]{3,2,1,0:T(8,128)S(1)}, u32[]{:S(2)}, u32[]{:S(2)}) collective-permute-start(f32[2,2,256,128]{3,2,1,0:T(8,128)S(1)} %collective-permute-done.12.refs_8_), channel_id=1, source_target_pairs={{1,0},{2,1},{3,2},{5,4},{6,5},{7,6},{9,8},{10,9},{11,10},{13,12},{... | collective-permute-start | bytes 1572872 | tf_op jit(solution)/shard_map/ppermute | solution.py:363
  391.1 27.4 %collective-permute-start.14 = (f32[2,2,256,128]{3,2,1,0:T(8,128)S(1)}, f32[2,2,256,128]{3,2,1,0:T(8,128)S(1)}, u32[]{:S(2)}, u32[]{:S(2)}) collective-permute-start(f32[2,2,256,128]{3,2,1,0:T(8,128)S(1)} %collective-permute-done.8.refs_4_), channel_id=1, source_target_pairs={{0,1},{1,2},{2,3},{4,5},{5,6},{6,7},{8,9},{9,10},{10,11},{12,13},{... | collective-permute-start | bytes 1572872 | tf_op jit(solution)/shard_map/ppermute | solution.py:362
  400.9 22.2 %collective-permute-start.17 = (f32[2,2,256,128]{3,2,1,0:T(8,128)S(1)}, f32[2,2,256,128]{3,2,1,0:T(8,128)S(1)}, u32[]{:S(2)}, u32[]{:S(2)}) collective-permute-start(f32[2,2,256,128]{3,2,1,0:T(8,128)S(1)} %collective-permute-done.13.refs_9_), channel_id=1, source_target_pairs={{1,0},{2,1},{3,2},{5,4},{6,5},{7,6},{9,8},{10,9},{11,10},{13,12},{... | collective-permute-start | bytes 1572872 | tf_op jit(solution)/shard_map/ppermute | solution.py:363
  (28 other events, 347.0 us)
